TPU v7x, 32 devices: a whole 2x2x4 slice. The times are simulated.
32 devices in a mesh: dp: 8 (over z, y), row: 2 (over x), col: 2 (over core).
Axes of the slice: x: 2, y: 2, z: 4, core: 2. Of those that a mesh axis runs over, the one named last changes fastest.
Arguments:
- stream: bfloat16 [4096, 2560], P(('dp', 'row'), 'col'), may hold values from -45 to 45
- scale_first: float32 [2560], P('col'), may hold values from -0.5 to 0.5
- branch_weight: bfloat16 [2560, 2560], P('col', ('row', 'dp')), may hold values from -0.125 to 0.125
- branch_bias: float32 [2560], P('row'), may hold values from -3 to 3
- mixer_weight: bfloat16 [2560, 2560], P('col', ('row', 'dp')), may hold values from -0.125 to 0.125
- mixer_bias: float32 [2560], P('row'), may hold values from -3 to 3
- conv_weight: float32 [4, 2560], P(None, 'row'), may hold values from -3 to 3
- conv_bias: float32 [2560], P('row'), may hold values from -2 to 2
- decay_weight: bfloat16 [10, 256, 256], P('row'), may hold values from -0.375 to 0.375
- decay_bias: float32 [2560], P('row'), may hold values from -3 to 3
- input_weight: bfloat16 [10, 256, 256], P('row'), may hold values from -0.375 to 0.375
- input_bias: float32 [2560], P('row'), may hold values from -3 to 3
- decay_param: float32 [2560], P('row'), may hold values from -13 to -4
- output_weight: bfloat16 [2560, 2560], P('row', ('col', 'dp')), may hold values from -0.3125 to 0.3125
- output_bias: float32 [2560], P('col'), may hold values from -3 to 3
- scale_second: float32 [2560], P('col'), may hold values from -0.5 to 0.5
- gate_weight: bfloat16 [2560, 7680], P('col', ('row', 'dp')), may hold values from -0.125 to 0.125
- gate_bias: float32 [7680], P('row'), may hold values from -3 to 3
- up_weight: bfloat16 [2560, 7680], P('col', ('row', 'dp')), may hold values from -0.125 to 0.125
- up_bias: float32 [7680], P('row'), may hold values from -3 to 3
- down_weight: bfloat16 [7680, 2560], P('row', ('col', 'dp')), may hold values from -0.09375 to 0.09375
- down_bias: float32 [2560], P('col'), may hold values from -3 to 3
- cotangent: bfloat16 [4096, 2560], P(('dp', 'row'), 'col'), may hold values from -6 to 6
Outputs:
- result: bfloat16 [4096, 2560], P(('dp', 'row'), 'col')
- grad_stream: float32 [4096, 2560], P(('dp', 'row'), 'col')
- grad_scale_first: float32 [2560], P('col')
- grad_branch_weight: float32 [2560, 2560], P('col', ('row', 'dp'))
- grad_branch_bias: float32 [2560], P('row')
- grad_mixer_weight: float32 [2560, 2560], P('col', ('row', 'dp'))
- grad_mixer_bias: float32 [2560], P('row')
- grad_conv_weight: float32 [4, 2560], P(None, 'row')
- grad_conv_bias: float32 [2560], P('row')
- grad_decay_weight: float32 [10, 256, 256], P('row')
- grad_decay_bias: float32 [2560], P('row')
- grad_input_weight: float32 [10, 256, 256], P('row')
- grad_input_bias: float32 [2560], P('row')
- grad_decay_param: float32 [2560], P('row')
- grad_output_weight: float32 [2560, 2560], P('row', ('col', 'dp'))
- grad_output_bias: float32 [2560], P('col')
- grad_scale_second: float32 [2560], P('col')
- grad_gate_weight: float32 [2560, 7680], P('col', ('row', 'dp'))
- grad_gate_bias: float32 [7680], P('row')
- grad_up_weight: float32 [2560, 7680], P('col', ('row', 'dp'))
- grad_up_bias: float32 [7680], P('row')
- grad_down_weight: float32 [7680, 2560], P('row', ('col', 'dp'))
- grad_down_bias: float32 [2560], P('col')
All inputs are finite; a program needn't handle non-finite values.
Results may differ from a plain program's by a relative error of at most 0.022.
Values may be sent and summed in bfloat16 or wider, within the bound.
A program may use at most 320 MiB of HBM per device.

v0:
```python
import jax
import jax.numpy as jnp
from jax import lax
from jax.experimental import pallas as pl
from jax.experimental.pallas import tpu as pltpu
from jax.sharding import Mesh, PartitionSpec as P


D = 2560
CONV = 4
LEN = 4096
EPSILON = 1e-06
SQRT_FLOOR = 0.0001
TEAM = 4
NT = (((1,), (1,)), ((), ()))
TN = (((0,), (0,)), ((), ()))
F32 = jnp.float32
BF16 = jnp.bfloat16
DP = ("t", "f")
ORDER = ("t", "f", "col")


def dot_nn(a, b):
    return jnp.dot(a, b, preferred_element_type=F32)


def dot_nt(a, b):
    return lax.dot_general(a, b, NT, preferred_element_type=F32)


def dot_tn(a, b):
    return lax.dot_general(a, b, TN, preferred_element_type=F32)


MESH = pl.DeviceIdType.MESH
ANY = pl.BlockSpec(memory_space=pl.ANY)
VMEM = pl.BlockSpec(memory_space=pltpu.VMEM)


def peer_of(axis, k):
    n, me = lax.axis_size(axis), lax.axis_index(axis)
    if k == 0:
        return me
    if n == 2:
        return 1 - me
    if n == 4:
        return (me + 1 - 2 * (me % 2), (me + 2) % 4, 3 - me)[k - 1]
    return (me + k) % n


def source_of(axis, k):
    n, me = lax.axis_size(axis), lax.axis_index(axis)
    return peer_of(axis, k) if n in (2, 4) else (me + n - k) % n


def offsets(axis):
    n = lax.axis_size(axis)
    return (1, 3, 2) if n == 4 else tuple(range(1, n))


def grid_of(axes, far_first=False):
    grid = [()]
    for axis in axes:
        near = (0,) + offsets(axis)
        grid = [tag + (k,) for tag in grid for k in (near[::-1] if far_first else near)]
    return grid


def hail(peers):
    for peer in peers:
        pl.semaphore_signal(pltpu.get_barrier_semaphore(), inc=1, device_id=peer, device_id_type=MESH)


def greet(peers):
    hail(peers)
    pl.semaphore_wait(pltpu.get_barrier_semaphore(), len(peers))


def only(condition, act):
    if condition is None:
        act()
    else:
        pl.when(condition)(act)


def along(*axes):
    return [{axis: peer_of(axis, k)} for axis in axes for k in offsets(axis)]


def across(*axes):
    return [
        {axis: peer_of(axis, k) for axis, k in zip(axes, tag)} for tag in grid_of(axes) if any(tag)
    ]


class Copies:
    def __init__(self):
        self.sent = []

    def push(self, src, dst, send, recv, peer, condition=None):
        copy = pltpu.make_async_remote_copy(
            src_ref=src, dst_ref=dst, send_sem=send, recv_sem=recv, device_id=peer, device_id_type=MESH
        )
        only(condition, copy.start)
        self.sent.append((condition, copy.wait_send))

    def arrive(self, dst, send, recv, peer):
        pltpu.make_async_remote_copy(
            src_ref=dst, dst_ref=dst, send_sem=send, recv_sem=recv, device_id=peer, device_id_type=MESH
        ).wait_recv()

    def keep(self, src, dst, sem):
        copy = pltpu.make_async_copy(src, dst, sem)
        copy.start()
        self.sent.append((None, copy.wait))

    def drain(self):
        for condition, wait in self.sent:
            only(condition, wait)


def leading(ref, coords):
    return ref.at[tuple(coords)]


class Gather(Copies):
    def __init__(self, src, out, axes, sems, place=leading):
        super().__init__()
        self.src, self.out, self.axes, self.place = src, out, axes, place
        self.send, self.recv, self.own = sems
        self.size, self.at = lax.axis_size(axes[0]), lax.axis_index(axes[0])
        self.nobody = (0,) * len(axes)
        self.waves = {}
        line = [0] + [v for far in range(1, self.size) for v in (-far, far)]
        for v in line:
            for rest in grid_of(axes[1:]):
                tag = (v,) + rest
                if any(tag):
                    self.waves.setdefault(sum(1 for k in tag if k), []).append(tag)

    @staticmethod
    def scratch(axes):
        sizes = [lax.axis_size(a) for a in axes]
        shape = (2 * sizes[0] - 1,) + tuple(sizes[1:])
        return [pltpu.SemaphoreType.DMA(shape), pltpu.SemaphoreType.DMA(shape), pltpu.SemaphoreType.DMA]

    def index(self, tag):
        return (tag[0] + self.size - 1,) + tag[1:]

    def exists(self, far):
        if far == 0:
            return None
        return self.at + far >= 0 if far < 0 else self.at + far < self.size

    def slot(self, tag):
        rest = [source_of(a, k) for a, k in zip(self.axes[1:], tag[1:])]
        return self.place(self.out, [self.at + tag[0]] + rest)

    def spread(self, tag):
        last = max([i for i, k in enumerate(tag) if k], default=-1)
        here = self.exists(tag[0])
        src = self.slot(tag) if any(tag) else self.src

        def send(there, peer, condition):
            if here is not None and condition is not None:
                condition = here & condition
            elif condition is None:
                condition = here
            at = self.index(there)
            self.push(src, self.slot(tag), self.send.at[at], self.recv.at[at], peer, condition)

        if last <= 0:
            if 0 <= tag[0] < self.size - 1:
                send((tag[0] + 1,) + tag[1:], {self.axes[0]: self.at - 1}, self.at > 0)
            if -self.size + 1 < tag[0] <= 0:
                send((tag[0] - 1,) + tag[1:], {self.axes[0]: self.at + 1}, self.at < self.size - 1)
        for level in range(max(last, 0) + 1, len(self.axes)):
            axis = self.axes[level]
            for k in offsets(axis):
                send(tag[:level] + (k,) + tag[level + 1 :], {axis: peer_of(axis, k)}, None)

    def begin(self):
        self.spread(self.nobody)
        self.keep(self.src, self.slot(self.nobody), self.own)

    def stage(self, wave):
        for tag in self.waves.get(wave, ()):
            last = max(i for i, k in enumerate(tag) if k)
            if last:
                peer = {self.axes[last]: peer_of(self.axes[last], tag[last])}
            else:
                peer = {self.axes[0]: self.at + (1 if tag[0] > 0 else -1)}
            at = self.index(tag)
            only(
                self.exists(tag[0]),
                lambda: self.arrive(self.slot(tag), self.send.at[at], self.recv.at[at], peer),
            )
            self.spread(tag)


def sum_into(out, parts):
    rows = out.shape[0]
    step = next(n for n in (32, 16, 8, rows) if rows % n == 0)

    def some(i, carry):
        at = pl.ds(pl.multiple_of(i * step, step), step)
        total = parts[0][at, :].astype(F32)
        for part in parts[1:]:
            total = total + part[at, :].astype(F32)
        out[at, :] = total.astype(out.dtype)
        return carry

    lax.fori_loop(0, rows // step, some, 0)


class Reduce(Copies):
    def __init__(self, src, out, axes, scratch, place=leading):
        super().__init__()
        n = len(axes)
        self.src, self.out, self.axes, self.place = src, out, axes, place
        self.part = {i + 1: scratch[i] for i in range(n - 1)}
        rest = scratch[n - 1 :]
        self.come = rest[:n]
        self.send = rest[n : 2 * n]
        self.recv = rest[2 * n : 3 * n]

    @staticmethod
    def count(axes):
        return 4 * len(axes) - 1

    @staticmethod
    def scratch(axes, block, dtype):
        sizes = tuple(lax.axis_size(a) for a in axes)
        n = len(axes)
        parts = [pltpu.VMEM(sizes[:i] + block, dtype) for i in range(1, n)]
        come = [pltpu.VMEM((sizes[i] - 1,) + sizes[:i] + block, dtype) for i in range(n)]
        sems = [pltpu.SemaphoreType.DMA((sizes[i] - 1,) + sizes[:i]) for i in range(n)]
        return parts + come + sems + sems

    def coords(self, tag):
        return tuple(peer_of(a, k) for a, k in zip(self.axes, tag))

    def forward(self, tag, src):
        level = len(tag) - 1
        k, prefix = tag[-1], tag[:-1]
        axis = self.axes[level]
        self.push(
            src,
            self.come[level].at[(k - 1,) + self.coords(prefix)],
            self.send[level].at[(k - 1,) + prefix],
            self.recv[level].at[(k - 1,) + prefix],
            {axis: peer_of(axis, k)},
        )

    def order(self, level):
        return sorted(grid_of(self.axes[:level], True), key=lambda tag: tag[-1:] == (0,))

    def begin(self):
        for tag in self.order(len(self.axes)):
            if tag[-1]:
                self.forward(tag, self.place(self.src, self.coords(tag)))

    def held(self, level, coords):
        return self.place(self.src, coords) if level == len(self.axes) else self.part[level].at[coords]

    def step(self, level, tag):
        axis = self.axes[level]
        here = self.coords(tag)
        parts = [self.held(level + 1, here + (lax.axis_index(axis),))]
        for k in offsets(axis):
            slot = self.come[level].at[(k - 1,) + here]
            at = (k - 1,) + tag
            self.arrive(slot, self.send[level].at[at], self.recv[level].at[at], {axis: source_of(axis, k)})
            parts.append(slot)
        target = self.held(level, here) if level else self.out
        sum_into(target, parts)
        if level and tag[-1]:
            self.forward(tag, target)

    def stage(self, wave):
        level = len(self.axes) - wave
        if level >= 0:
            for tag in self.order(level):
                self.step(level, tag)


class Settle(Reduce):
    def __init__(self, src, out, axes, scratch, place):
        Copies.__init__(self)
        n = len(axes)
        self.src, self.out, self.axes, self.place = src, out, axes, place
        self.come, self.send, self.recv = scratch[:n], scratch[n : 2 * n], scratch[2 * n :]

    @staticmethod
    def scratch(axes, block, dtype):
        return Reduce.scratch(axes, block, dtype)[len(axes) - 1 :]

    def held(self, level, coords):
        return self.place(self.src, coords + tuple(lax.axis_index(a) for a in self.axes[level:]))


class Spread(Copies):
    def __init__(self, src, out, axes, sems):
        super().__init__()
        self.src, self.out, self.axes = src, out, axes
        self.send, self.recv, self.own = sems
        self.waves = {}
        for tag in grid_of(axes):
            if any(tag):
                self.waves.setdefault(sum(1 for k in tag if k), []).append(tag)

    @staticmethod
    def scratch(axes):
        shape = shape_of(axes)
        return [pltpu.SemaphoreType.DMA(shape), pltpu.SemaphoreType.DMA(shape), pltpu.SemaphoreType.DMA]

    def slot(self, tag):
        return self.out.at[tuple(source_of(a, k) for a, k in zip(self.axes, tag))]

    def spread(self, tag):
        last = max([i for i, k in enumerate(tag) if k], default=-1)
        for level in range(last + 1, len(self.axes)):
            axis = self.axes[level]
            for k in offsets(axis):
                at = tag[:level] + (k,) + tag[level + 1 :]
                src = self.slot(tag) if any(tag) else self.src
                self.push(src, self.slot(tag), self.send.at[at], self.recv.at[at], {axis: peer_of(axis, k)})

    def begin(self):
        nobody = (0,) * len(self.axes)
        self.spread(nobody)
        self.keep(self.src, self.slot(nobody), self.own)

    def stage(self, wave):
        for tag in self.waves.get(wave, ()):
            last = max(i for i, k in enumerate(tag) if k)
            peer = {self.axes[last]: peer_of(self.axes[last], tag[last])}
            self.arrive(self.slot(tag), self.send.at[tag], self.recv.at[tag], peer)
            self.spread(tag)


class Fan(Copies):
    def __init__(self, src, out, axis, sems):
        super().__init__()
        self.src, self.out, self.axis = src, out, axis
        self.send, self.recv, self.own = sems
        self.half = lax.axis_size(axis) // 2

    @staticmethod
    def scratch(axis):
        n = lax.axis_size(axis)
        return [pltpu.SemaphoreType.DMA((n,)), pltpu.SemaphoreType.DMA((n, 2)), pltpu.SemaphoreType.DMA]

    def slot(self, owner, core):
        width = self.src.shape[-1]
        return self.out.at[owner % self.half, :, pl.ds(pl.multiple_of(core * width, width), width)]

    def begin(self):
        me, core = lax.axis_index(self.axis), lax.axis_index("col")
        target = me // self.half
        slot = self.slot(me, core)
        self.copies = []
        for k in offsets(self.axis):
            peer = {self.axis: peer_of(self.axis, k), "col": target}
            for c in (0, 1):

                @pl.when(core == c)
                def _(c=c):
                    pltpu.make_async_remote_copy(
                        src_ref=self.src, dst_ref=slot, send_sem=self.send.at[k], recv_sem=self.recv.at[k, c],
                        device_id=peer, device_id_type=MESH,
                    ).start()

        @pl.when(target == core)
        def _():
            pltpu.make_async_copy(self.src, slot, self.own).start()

        for c in (0, 1):

            @pl.when((target != core) & (core == c))
            def _(c=c):
                pltpu.make_async_remote_copy(
                    src_ref=self.src, dst_ref=slot, send_sem=self.send.at[0], recv_sem=self.recv.at[0, c],
                    device_id={"col": 1 - core}, device_id_type=MESH,
                ).start()

    def stage(self, wave):
        if wave != 1:
            return
        me, core = lax.axis_index(self.axis), lax.axis_index("col")
        for k in (0,) + offsets(self.axis):
            owner = source_of(self.axis, k)
            for c in (0, 1):
                expected = owner // self.half == core
                if k == 0:
                    expected = expected & (core != c)

                @pl.when(expected)
                def _(k=k, c=c, owner=owner):
                    slot = self.slot(owner, c)
                    self.arrive(slot, self.send.at[k], self.recv.at[k, c], {self.axis: owner, "col": c} if k else {"col": 1 - core})

    def drain(self):
        me, core = lax.axis_index(self.axis), lax.axis_index("col")
        target = me // self.half
        slot = self.slot(me, core)

        def left(k, peer):
            pltpu.make_async_remote_copy(
                src_ref=self.src, dst_ref=slot, send_sem=self.send.at[k], recv_sem=self.recv.at[k, 0],
                device_id=peer, device_id_type=MESH,
            ).wait_send()

        for k in offsets(self.axis):
            left(k, {self.axis: peer_of(self.axis, k), "col": target})

        @pl.when(target == core)
        def _():
            pltpu.make_async_copy(self.src, slot, self.own).wait()

        @pl.when(target != core)
        def _():
            left(0, {"col": 1 - core})


class Fold(Copies):
    def __init__(self, src, out, axis, scratch):
        super().__init__()
        self.src, self.out, self.axis = src, out, axis
        self.come, self.send, self.recv, self.own = scratch
        self.half = lax.axis_size(axis) // 2

    @staticmethod
    def scratch(axis, block, dtype):
        n = lax.axis_size(axis)
        return [
            pltpu.VMEM((n,) + block, dtype),
            pltpu.SemaphoreType.DMA((n, 2)),
            pltpu.SemaphoreType.DMA((n,)),
            pltpu.SemaphoreType.DMA,
        ]

    def each(self, visit, cores=(0, 1)):
        me, core = lax.axis_index(self.axis), lax.axis_index("col")
        for k in offsets(self.axis) + (0,):
            owner = peer_of(self.axis, k)
            for c in cores:

                @pl.when(owner // self.half == core)
                def _(k=k, c=c, owner=owner):
                    piece = self.src.at[c, owner % self.half]
                    if k:
                        visit(k, c, piece, {self.axis: owner, "col": c})
                    else:

                        @pl.when(core == c)
                        def _():
                            visit(k, None, piece, None)

                        @pl.when(core != c)
                        def _():
                            visit(k, c, piece, {"col": 1 - core})

    def begin(self, cores=(0, 1)):
        def start(k, c, piece, peer):
            if peer is None:
                pltpu.make_async_copy(piece, self.come.at[k], self.own).start()
            else:
                pltpu.make_async_remote_copy(
                    src_ref=piece, dst_ref=self.come.at[k], send_sem=self.send.at[k, c], recv_sem=self.recv.at[k],
                    device_id=peer, device_id_type=MESH,
                ).start()

        self.each(start, cores)

    def stage(self, wave):
        if wave != 1:
            return
        me, core = lax.axis_index(self.axis), lax.axis_index("col")
        holder = me // self.half
        for k in offsets(self.axis):
            peer = {self.axis: source_of(self.axis, k), "col": holder}
            self.arrive(self.come.at[k], self.send.at[k, 0], self.recv.at[k], peer)

        @pl.when(holder != core)
        def _():
            self.arrive(self.come.at[0], self.send.at[0, 0], self.recv.at[0], {"col": 1 - core})

        @pl.when(holder == core)
        def _():
            pltpu.make_async_copy(self.src.at[0, 0], self.come.at[0], self.own).wait()

        sum_into(self.out, [self.come.at[k] for k in (0,) + offsets(self.axis)])

    def drain(self):
        def left(k, c, piece, peer):
            if peer is not None:
                pltpu.make_async_remote_copy(
                    src_ref=piece, dst_ref=self.come.at[k], send_sem=self.send.at[k, c], recv_sem=self.recv.at[k],
                    device_id=peer, device_id_type=MESH,
                ).wait_send()

        self.each(left)


class Trade(Copies):
    def __init__(self, src, out, scratch):
        super().__init__()
        self.src, self.out = src, out
        self.cut, self.send, self.recv, self.own = scratch

    @staticmethod
    def scratch(piece, dtype):
        shape = shape_of(("t", "col"))
        sems = [pltpu.SemaphoreType.DMA(shape), pltpu.SemaphoreType.DMA(shape), pltpu.SemaphoreType.DMA]
        return [pltpu.VMEM(shape + piece, dtype)] + sems

    def begin(self):
        share = self.cut.shape[-1]
        for i in range(2 * TEAM):
            self.cut[i // 2, i % 2] = self.src[:, i * share : (i + 1) * share]
        t, c = lax.axis_index("t"), lax.axis_index("col")
        for tag in grid_of(("t", "col")):
            to = peer_of("t", tag[0]), peer_of("col", tag[1])
            if any(tag):
                peer = {"t": to[0], "col": to[1]}
                self.push(self.cut.at[to], self.out.at[c, t], self.send.at[tag], self.recv.at[tag], peer)
        self.keep(self.cut.at[t, c], self.out.at[c, t], self.own)

    def stage(self, wave):
        if wave == 1:
            for tag in grid_of(("t", "col")):
                if any(tag):
                    peer = source_of("t", tag[0]), source_of("col", tag[1])
                    slot = self.out.at[peer[1], peer[0]]
                    self.arrive(slot, self.send.at[tag], self.recv.at[tag], {"t": peer[0], "col": peer[1]})


class Undeal(Copies):
    def __init__(self, src, out, scratch):
        super().__init__()
        self.src, self.out = src, out
        self.come, self.part, self.send, self.recv, self.send_on, self.recv_on, self.own = scratch

    @staticmethod
    def scratch(block, dtype):
        f, t, c = (lax.axis_size(a) for a in ("f", "t", "col"))
        first, second = pltpu.SemaphoreType.DMA((f - 1, t, c)), pltpu.SemaphoreType.DMA((t, c))
        return [
            pltpu.VMEM((f - 1, t, c) + block, dtype),
            pltpu.VMEM((t, c) + block, dtype),
            first, first, second, second, pltpu.SemaphoreType.DMA,
        ]

    def begin(self):
        for tag in grid_of(("t", "col"), True):
            to = peer_of("t", tag[0]), peer_of("col", tag[1])
            for k in offsets("f"):
                at = (k - 1,) + tag
                self.push(
                    self.src.at[(peer_of("f", k),) + to], self.come.at[(k - 1,) + to],
                    self.send.at[at], self.recv.at[at], {"f": peer_of("f", k)},
                )

    def stage(self, wave):
        t, c, f = (lax.axis_index(a) for a in ("t", "col", "f"))
        if wave == 1:
            for tag in grid_of(("t", "col"), True):
                to = peer_of("t", tag[0]), peer_of("col", tag[1])
                parts = [self.src.at[(f,) + to]]
                for k in offsets("f"):
                    at = (k - 1,) + tag
                    slot = self.come.at[(k - 1,) + to]
                    self.arrive(slot, self.send.at[at], self.recv.at[at], {"f": source_of("f", k)})
                    parts.append(slot)
                sum_into(self.part.at[to], parts)
                if any(tag):
                    self.push(
                        self.part.at[to], self.out.at[t, c], self.send_on.at[tag], self.recv_on.at[tag],
                        {"t": to[0], "col": to[1]},
                    )
                else:
                    self.keep(self.part.at[to], self.out.at[t, c], self.own)
        if wave == 2:
            for tag in grid_of(("t", "col")):
                if any(tag):
                    peer = source_of("t", tag[0]), source_of("col", tag[1])
                    self.arrive(
                        self.out.at[peer], self.send_on.at[tag], self.recv_on.at[tag], {"t": peer[0], "col": peer[1]}
                    )


def run_jobs(jobs, order):
    done = [-1] * len(jobs)
    for i in tuple(order) + tuple(range(len(jobs))) * 7:
        done[i] += 1
        if done[i]:
            jobs[i].stage(done[i])
        else:
            jobs[i].begin()
    for job in jobs:
        job.drain()


def exchange(cid, peers, plan, operands, out_shapes, out_spaces, order=(), through=None):
    n_in, n_out = len(operands), len(out_shapes)
    in_specs, aliases = [VMEM] * n_in, {}
    if through is not None:
        aliases[n_in] = n_out
        operands, in_specs = list(operands) + [through], in_specs + [ANY]
        out_shapes, out_spaces = list(out_shapes) + [like(through.shape, through.dtype)], list(out_spaces) + [ANY]
    scratch = [s for job in plan for s in job[4]]

    def kernel(*refs):
        n_op, n_res = len(in_specs), len(out_shapes)
        ins, outs, rest = refs[:n_in], refs[n_op : n_op + n_out], refs[n_op + n_res :]
        greet(peers())
        jobs = []
        for make, src, out, options, own in plan:
            mine, rest = rest[: len(own)], rest[len(own) :]
            jobs.append(make(ins[src], outs[out], *options[0], mine, **options[1]))
        run_jobs(jobs, order)

    return pl.pallas_call(
        kernel,
        out_shape=tuple(out_shapes),
        in_specs=in_specs,
        out_specs=tuple(out_spaces),
        scratch_shapes=scratch,
        input_output_aliases=aliases,
        compiler_params=pltpu.CompilerParams(collective_id=cid, has_side_effects=True),
    )(*operands)


class Swap(Copies):
    def __init__(self, src, out, sems):
        super().__init__()
        self.src, self.out = src, out
        self.send, self.recv = sems

    @staticmethod
    def scratch():
        return [pltpu.SemaphoreType.DMA, pltpu.SemaphoreType.DMA]

    def begin(self):
        other = 1 - lax.axis_index("col")
        self.push(self.src.at[other], self.out, self.send, self.recv, {"col": other})

    def stage(self, wave):
        if wave == 1:
            self.arrive(self.out, self.send, self.recv, {"col": 1 - lax.axis_index("col")})


class AllReduce(Copies):
    def __init__(self, src, out, axes, scratch):
        super().__init__()
        n = Reduce.count(axes)
        self.depth = len(axes)
        self.reduce = Reduce(src, scratch[n], axes, scratch[:n])
        self.gather = Spread(scratch[n], out, axes, scratch[n + 1 :])

    @staticmethod
    def scratch(axes, block, dtype):
        return Reduce.scratch(axes, block, dtype) + [pltpu.VMEM(block, dtype)] + Spread.scratch(axes)

    def begin(self):
        self.reduce.begin()

    def stage(self, wave):
        if wave <= self.depth:
            self.reduce.stage(wave)
        if wave == self.depth:
            self.gather.begin()
        if wave > self.depth:
            self.gather.stage(wave - self.depth)

    def drain(self):
        self.reduce.drain()
        self.gather.drain()


def shape_of(axes):
    return tuple(lax.axis_size(a) for a in axes)


def lanes_of(width):
    def place(ref, coords):
        return ref.at[tuple(coords[:-1]) + (slice(None), pl.ds(pl.multiple_of(coords[-1] * width, width), width))]

    return place


def col_first(ref, coords):
    return ref.at[(coords[-1],) + tuple(coords[:-1])]


def like(shape, dtype):
    return jax.ShapeDtypeStruct(shape, dtype)


def pair_sum(values, cid, through=None):
    share = 128 // len(values)
    wide = jnp.concatenate([jnp.broadcast_to(v, (v.shape[0], share)) for v in values], axis=1)
    both, *passed = exchange(
        cid, lambda: along("col"),
        [(Gather, 0, 0, ((PAIR,), {}), Gather.scratch(PAIR))],
        [wide], [like((2,) + wide.shape, F32)], [VMEM], through=through,
    )
    total = both[0] + both[1]
    return [total[:, i * share : i * share + 1] for i in range(len(values))] + passed


def recurrence(retain, source, lead, backward, cid):
    rows, width = retain.shape
    tiles = rows // 8
    sizes = shape_of(ORDER)
    count = sizes[0] * sizes[1] * sizes[2]
    lines = width // 128
    block = (-(-2 * lines // 8) * 8, 128)

    def kernel(r_ref, s_ref, lead_ref, h_ref, in_ref, c_ref, mine, ends, send, recv, own):
        peers = across(*ORDER)
        hail(peers)
        row = lax.broadcasted_iota(jnp.int32, (8, width), 0)

        def tile(i):
            return pl.ds(pl.multiple_of(8 * (tiles - 1 - i if backward else i), 8), 8)

        def step(i, carry):
            decay, state = carry
            at = tile(i)
            r, s = r_ref[at, :], s_ref[at, :]
            for by in (1, 2, 4):
                keep = row < 8 - by if backward else row >= by
                shift = 8 - by if backward else by
                r_by = jnp.where(keep, pltpu.roll(r, shift, 0), 1.0)
                s_by = jnp.where(keep, pltpu.roll(s, shift, 0), 0.0)
                s = r * s_by + s
                r = r * r_by
            s = s + r * state
            r = r * decay
            c_ref[at, :] = r
            h_ref[at, :] = s
            end = 0 if backward else 7
            return r[end : end + 1, :], s[end : end + 1, :]

        one = jnp.ones((1, width), F32)
        decay, state = lax.fori_loop(0, tiles, step, (one, jnp.zeros((1, width), F32)))
        decay, state = lead_ref[0:1, :] * decay, lead_ref[0:1, :] * state
        for j in range(lines):
            mine[j : j + 1, :] = decay[:, 128 * j : 128 * (j + 1)]
            mine[lines + j : lines + j + 1, :] = state[:, 128 * j : 128 * (j + 1)]
        pl.semaphore_wait(pltpu.get_barrier_semaphore(), len(peers))
        jobs = Copies()
        here = tuple(lax.axis_index(a) for a in ORDER)
        for tag in grid_of(ORDER):
            if any(tag):
                peer = {a: peer_of(a, k) for a, k in zip(ORDER, tag)}
                jobs.push(mine, ends.at[here], send.at[tag], recv.at[tag], peer)
        jobs.keep(mine, ends.at[here], own)
        for tag in grid_of(ORDER):
            if any(tag):
                peer = {a: source_of(a, k) for a, k in zip(ORDER, tag)}
                jobs.arrive(ends.at[tuple(peer[a] for a in ORDER)], send.at[tag], recv.at[tag], peer)
        jobs.drain()
        me = (here[0] * sizes[1] + here[1]) * sizes[2] + here[2]
        entering = jnp.zeros((lines, 128), F32)
        for i in range(count):
            peer = count - 1 - i if backward else i
            t, rest = divmod(peer, sizes[1] * sizes[2])
            f, c = divmod(rest, sizes[2])
            pair = ends[t, f, c]
            ahead = jnp.where(peer > me if backward else peer < me, 1, 0)
            entering = jnp.where(ahead == 1, pair[:lines] * entering + pair[lines : 2 * lines], entering)
        entering = jnp.concatenate([entering[j : j + 1, :] for j in range(lines)], axis=1)
        in_ref[...] = jnp.broadcast_to(entering, (8, width))

        def fix(i, carry):
            at = tile(i)
            h_ref[at, :] = h_ref[at, :] + c_ref[at, :] * entering
            return carry

        lax.fori_loop(0, tiles, fix, 0)

    states, entering = pl.pallas_call(
        kernel,
        out_shape=(like((rows, width), F32), like((8, width), F32)),
        in_specs=[VMEM] * 3,
        out_specs=(VMEM, VMEM),
        scratch_shapes=[
            pltpu.VMEM((rows, width), F32),
            pltpu.VMEM(block, F32),
            pltpu.VMEM(sizes + block, F32),
            pltpu.SemaphoreType.DMA(sizes),
            pltpu.SemaphoreType.DMA(sizes),
            pltpu.SemaphoreType.DMA,
        ],
        compiler_params=pltpu.CompilerParams(collective_id=cid, has_side_effects=True),
        name="back_states" if backward else "states",
    )(retain, source, jnp.broadcast_to(lead, (8, width)))
    return states, entering[0]


def from_behind(x, axis, by):
    peers = lax.axis_size(axis)
    pairs = [(i, i + by) for i in range(peers) if 0 <= i + by < peers]
    return lax.ppermute(x, axis, pairs)


def gelu_tanh(values):
    return jax.nn.gelu(values, approximate=True)


def gates_of(decay_pre, input_pre, decay_param, conv_low, starts):
    rate_gate = jax.nn.sigmoid(decay_pre)
    in_gate = jax.nn.sigmoid(input_pre)
    log_decay = -8.0 * jax.nn.softplus(decay_param) * rate_gate
    retain = jnp.where(starts, 0.0, jnp.exp(log_decay))
    multiplier = jnp.where(
        starts, 1.0, jnp.sqrt(jnp.maximum(-jnp.expm1(2.0 * log_decay), SQRT_FLOOR))
    )
    return (retain, multiplier * in_gate * conv_low)


def normalize_back(gradient, values, inverse, scale_vec, cid, through=None):
    weighted = gradient * (1.0 + scale_vec)
    scale_grad = jnp.sum(gradient * values * inverse, axis=0)
    inner_sum, *passed = pair_sum([jnp.sum(weighted * values, axis=1, keepdims=True)], cid, through)
    return (inverse * weighted - values * inverse**3 * inner_sum / D, scale_grad, *passed)


def arrange(own, other):
    first = lax.axis_index("col") == 0
    return jnp.where(first, own, other), jnp.where(first, other, own)


def halves(x):
    width = x.shape[1] // 2
    return jnp.stack([x[:, :width], x[:, width:]])


def half_of(x):
    width = x.shape[1] // 2
    return jnp.where(lax.axis_index("col") == 0, x[:, :width], x[:, width:])


TOKEN_AXES = ("t", "row", "col")
WEIGHT_AXES = ("t", "f", "col")
PAIR = ("col",)


def fetch_first(mixer, branch, output, stream, scale, down):
    t, f, c = shape_of(WEIGHT_AXES)
    width, inner = mixer.shape
    piece = (down.shape[0], down.shape[1] // (2 * TEAM))
    place = lanes_of(inner)
    axes = (WEIGHT_AXES,)
    plan = [
        (Gather, 0, 0, (axes, {"place": place}), Gather.scratch(WEIGHT_AXES)),
        (Fan, 3, 3, (("row",), {}), Fan.scratch("row")),
        (Gather, 1, 1, (axes, {"place": place}), Gather.scratch(WEIGHT_AXES)),
        (Gather, 2, 2, (axes, {"place": col_first}), Gather.scratch(WEIGHT_AXES)),
        (Gather, 4, 4, ((PAIR,), {}), Gather.scratch(PAIR)),
        (Trade, 5, 5, ((), {}), Trade.scratch(piece, BF16)),
    ]
    wide = like((t, f, width, 2 * inner), BF16)
    outs = [wide, wide, like((c, t, f) + output.shape, BF16), like((1, stream.shape[0], 2 * stream.shape[1]), BF16)]
    outs += [like((2, 1, scale.shape[0]), F32), like((2, TEAM) + piece, BF16)]
    mixer_t, branch_t, output_t, tokens, scale, down = exchange(
        0, lambda: along("t", "f") + across("row", "col") + diagonal("t", "col"), plan,
        [mixer, branch, output, stream, scale[None], down], outs, [ANY] * 4 + [VMEM, ANY],
        order=(0, 1, 2, 3, 4, 0, 5, 2, 3),
    )
    return mixer_t.reshape(-1, 2 * inner), branch_t.reshape(-1, 2 * inner), output_t.reshape(-1, output.shape[1]), tokens[0], scale.reshape(-1), down


def fetch_second(normed, cotangent, gate, up, down):
    t, r, _ = shape_of(TOKEN_AXES)
    fleet = lax.axis_size("f")
    rows, width = normed.shape
    units, inner = gate.shape
    share = down.shape[-1]
    half = fleet // 2
    token, fan = Gather.scratch(TOKEN_AXES), Fan.scratch("f")
    place = lanes_of(width)

    def kernel(n_ref, c_ref, g_ref, u_ref, d_ref, n_all, c_all, gw, uw, d_all, g_out, u_out, held, sem, *rest):
        normed_job = Gather(n_ref, n_all, TOKEN_AXES, rest[:3], place)
        cot_job = Gather(c_ref, c_all, TOKEN_AXES, rest[3:6], place)
        gate_job, up_job = Fan(g_ref, gw, "f", rest[6:9]), Fan(u_ref, uw, "f", rest[9:12])
        down_job = Gather(d_ref, d_all, ("f",), rest[12:15], lambda ref, at: ref.at[:, :, at[0]])
        jobs = (normed_job, gate_job, up_job, down_job, cot_job)
        greet(along("t", "row") + across("f", "col"))
        for job in jobs:
            job.begin()
        normed_job.stage(1)
        cot_job.stage(1)
        normed_job.stage(2)
        normed_job.stage(3)
        normed_job.drain()
        for job in (gate_job, up_job):
            job.stage(1)
            job.drain()
        blocks = t * r

        def fetch(i):
            return pltpu.make_async_copy(n_all.at[i // r, i % r], held.at[i % 2], sem.at[i % 2])

        fetch(0).start()

        def product(i, carry):
            @pl.when(i + 1 < blocks)
            def _():
                fetch(i + 1).start()

            fetch(i).wait()
            at = pl.ds(pl.multiple_of(i * rows, rows), rows)
            for weight, out in ((gw, g_out), (uw, u_out)):
                for j in range(half):
                    out[at, j * units : (j + 1) * units] = dot_nt(held[i % 2], weight[j])
            return carry

        lax.fori_loop(0, blocks, product, 0)
        cot_job.stage(2)
        down_job.stage(1)
        cot_job.stage(3)
        for job in (down_job, cot_job):
            job.drain()

    every = like((t, r, rows, 2 * width), BF16)
    weight = like((half, units, 2 * inner), BF16)
    first = like((t * r * rows, share), F32)
    n_all, c_all, gate_t, up_t, down_t, gate_out, up_out = pl.pallas_call(
        kernel,
        out_shape=(every, every, weight, weight, like(down.shape[:2] + (fleet,) + down.shape[2:], BF16), first, first),
        in_specs=[VMEM] * 5,
        out_specs=(ANY, ANY, VMEM, VMEM, ANY, VMEM, VMEM),
        scratch_shapes=[pltpu.VMEM((2, rows, 2 * width), BF16), pltpu.SemaphoreType.DMA((2,))]
        + token + token + fan + fan + Gather.scratch(("f",)),
        compiler_params=pltpu.CompilerParams(collective_id=1, has_side_effects=True),
        name="fetch_second",
    )(normed, cotangent, gate, up, down)
    return (
        n_all.reshape(-1, 2 * width),
        c_all.reshape(-1, 2 * width),
        gate_t.reshape(-1, 2 * inner),
        up_t.reshape(-1, 2 * inner),
        down_t.reshape(-1, share),
        gate_out,
        up_out,
    )


def diagonal(*axes):
    pairs = zip(across(*axes), [tag for tag in grid_of(axes) if any(tag)])
    return [peer for peer, tag in pairs if all(tag)]


def team_peers():
    return along("t", "row") + across("f", "col") + diagonal("t", "col")


def send_second(gate, up, hidden, gate_t, up_t, second_all, cot_all, late):
    t, r, _ = shape_of(TOKEN_AXES)
    fleet = lax.axis_size("f")
    tokens, wide = second_all.shape
    share = gate.shape[1]
    rows, width = tokens // (t * r), wide // 2
    half = fleet // 2
    units = share // half
    shard = width // (TEAM * fleet)
    block, weight, piece = (rows, width), (units, width), (shard, share)
    lane, tile = 512, wide // 4
    part, chunk = tile // shard, 256
    place = lanes_of(width)
    settle, fold = Settle.scratch(TOKEN_AXES, block, BF16), Fold.scratch("f", weight, BF16)
    undeal = Undeal.scratch(piece, BF16)

    def kernel(*refs):
        g_ref, u_ref, h_ref, gw_ref, uw_ref, all_ref, cot_ref, _ = refs[:8]
        delta_ref, grad_g, grad_u, grad_d = refs[8:12]
        src, fold_g, fold_u, down, gt_ref, ut_ref, ht_ref, tiles, tile_sem = refs[12:21]
        rest = refs[21:]
        sums = Settle(src, delta_ref, TOKEN_AXES, rest[: len(settle)], place)
        rest = rest[len(settle) :]
        g_job = Fold(fold_g, grad_g, "f", rest[: len(fold)])
        u_job = Fold(fold_u, grad_u, "f", rest[len(fold) : 2 * len(fold)])
        d_job = Undeal(down, grad_d, rest[2 * len(fold) :])

        def fetch(ref, i):
            at = pl.ds(pl.multiple_of(i * tile, tile), tile)
            return pltpu.make_async_copy(ref.at[:, at], tiles.at[i % 2], tile_sem.at[i % 2])

        def turn(src_ref, out_ref):
            def some(i, carry):
                at = pl.ds(pl.multiple_of(i * chunk, chunk), chunk)
                out_ref[:, at] = src_ref[at, :].T
                return carry

            lax.fori_loop(0, tokens // chunk, some, 0)

        def down_gradients(i, carry):
            @pl.when(i + 1 < wide // tile)
            def _():
                fetch(cot_ref, i + 1).start()

            @pl.when(i + 1 == wide // tile)
            def _():
                fetch(all_ref, 0).start()

            fetch(cot_ref, i).wait()
            value = dot_nn(ht_ref[...], tiles[i % 2]).T.astype(BF16)
            for j in range(part):
                n = i * part + j
                down[n % fleet, n // fleet % TEAM, n // (TEAM * fleet)] = value[j * shard : (j + 1) * shard]
            return carry

        fetch(cot_ref, 0).start()
        turn(h_ref, ht_ref)
        greet(team_peers())
        lax.fori_loop(0, wide // tile, down_gradients, 0)
        d_job.begin()
        before = None
        for tag in sums.order(2):
            coords = sums.coords(tag)
            at = pl.ds(pl.multiple_of((coords[0] * r + coords[1]) * rows, rows), rows)

            def product(j, carry, at=at, coords=coords):
                col = pl.ds(pl.multiple_of(j * lane, lane), lane)
                value = dot_nn(g_ref[at, :], gw_ref[:, col]) + dot_nn(u_ref[at, :], uw_ref[:, col])
                src[coords[0], coords[1], :, col] = value.astype(BF16)
                return carry

            lax.fori_loop(0, wide // lane, product, 0)
            for k in offsets("col"):
                sums.forward(tag + (k,), place(src, sums.coords(tag + (k,))))
            if before is not None:
                sums.step(2, before)
            before = tag
        sums.step(2, before)
        middle = sums.order(1)
        sums.step(1, middle[0])
        d_job.stage(1)

        def gradients(i, carry):
            @pl.when(i + 1 < wide // tile)
            def _():
                fetch(all_ref, i + 1).start()

            fetch(all_ref, i).wait()
            h, at = i // (width // tile), pl.ds(pl.multiple_of(i % (width // tile) * tile, tile), tile)
            for left, out in ((gt_ref, fold_g), (ut_ref, fold_u)):
                value = dot_nn(left[...], tiles[i % 2]).astype(BF16)
                for j in range(half):
                    out[h, j, :, at] = value[j * units : (j + 1) * units]
            return carry

        turn(g_ref, gt_ref)
        turn(u_ref, ut_ref)
        for h in (0, 1):
            first = h * (width // tile)
            lax.fori_loop(first, first + width // tile, gradients, 0)
            g_job.begin((h,))
            u_job.begin((h,))
            sums.step(1, middle[1 + h])
        for tag in middle[3:]:
            sums.step(1, tag)
        sums.stage(3)
        g_job.stage(1)
        u_job.stage(1)
        d_job.stage(2)
        for job in (sums, g_job, u_job, d_job):
            job.drain()

    delta, grad_gate, grad_up, grad_down = pl.pallas_call(
        kernel,
        out_shape=(like(block, F32), like(weight, BF16), like(weight, BF16), like((TEAM, 2) + piece, BF16)),
        in_specs=[VMEM] * 5 + [ANY] * 3,
        out_specs=(VMEM,) * 4,
        scratch_shapes=[
            pltpu.VMEM((t, r, rows, wide), BF16),
            pltpu.VMEM((2, half) + weight, BF16),
            pltpu.VMEM((2, half) + weight, BF16),
            pltpu.VMEM((fleet, TEAM, 2) + piece, BF16),
            pltpu.VMEM((share, tokens), BF16),
            pltpu.VMEM((share, tokens), BF16),
            pltpu.VMEM((share, tokens), BF16),
            pltpu.VMEM((2, tokens, tile), BF16),
            pltpu.SemaphoreType.DMA((2,)),
        ]
        + settle + fold + fold + undeal,
        compiler_params=pltpu.CompilerParams(
            collective_id=2, has_side_effects=True, vmem_limit_bytes=67_000_000
        ),
        name="send_second",
    )(gate, up, hidden, gate_t, up_t, second_all, cot_all, late)
    grad_down = grad_down.reshape(2 * TEAM, shard, share).transpose(0, 2, 1).reshape(-1, shard)
    return delta, grad_gate, grad_up, grad_down


def to_stream(partial, cid):
    rows, width = partial.shape
    block = (rows, width // 2)
    (out,) = exchange(
        cid, lambda: across("row", "col"),
        [(Fold, 0, 0, (("row",), {}), Fold.scratch("row", block, BF16))],
        [halves(partial).reshape((2, 1) + block)], [like(block, F32)], [VMEM],
    )
    return out


def to_tokens(block, mixed, through, cid):
    rows, width = block.shape
    out, both, through = exchange(
        cid, lambda: across("row", "col"),
        [
            (Fan, 0, 0, (("row",), {}), Fan.scratch("row")),
            (Gather, 1, 1, ((PAIR,), {}), Gather.scratch(PAIR)),
        ],
        [block, mixed], [like((1, rows, 2 * width), BF16), like((2,) + mixed.shape, BF16)], [VMEM] * 2,
        through=through,
    )
    return out[0], both.reshape(-1, mixed.shape[1]), through


def core_rows(x, cid):
    (other,) = exchange(
        cid, lambda: along("col"), [(Swap, 0, 0, ((), {}), Swap.scratch())], [halves(x)],
        [like((x.shape[0], x.shape[1] // 2), x.dtype)], [VMEM],
    )
    return jnp.concatenate(arrange(half_of(x), other), axis=0)


def dealt(x, axes, dtype):
    sizes = shape_of(axes)
    members = sizes[0] * sizes[1] * sizes[2]
    width = -(-x.size // (members * 8 * 128)) * 128
    flat = jnp.pad(x.reshape(-1), (0, members * 8 * width - x.size))
    return flat.reshape(sizes + (8, width)).astype(dtype)


STREAM_AXES = ("t", "f", "row")


def finish_block(normed, branch, mixer, delta, cid):
    rows, width = delta.shape
    token = (rows, width // 2)
    plan = [
        (Fold, 0, 0, (("row",), {}), Fold.scratch("row", token, BF16)),
        (Swap, 1, 1, ((), {}), Swap.scratch()),
        (Gather, 2, 2, ((PAIR,), {}), Gather.scratch(PAIR)),
        (Gather, 3, 3, ((PAIR,), {}), Gather.scratch(PAIR)),
    ]
    outs = [like(token, F32), like(token, BF16), like((2,) + branch.shape, BF16), like((2,) + mixer.shape, BF16)]
    delta, other, branch, mixer = exchange(
        cid, lambda: across("row", "col"), plan,
        [halves(delta).reshape((2, 1) + token), halves(normed), branch, mixer], outs, [VMEM] * 4,
    )
    rows = jnp.concatenate(arrange(half_of(normed), other), axis=0)
    return delta, rows, branch.reshape(-1, branch.shape[2]), mixer.reshape(-1, mixer.shape[2])


def send_first(grads, inner_sums, head_grads, stream_sums, through, cid):
    sizes = shape_of(DP)
    n = len(grads)
    block = (grads[0].shape[0] // (sizes[0] * sizes[1]), grads[0].shape[1])
    axes_of = (ORDER, STREAM_AXES, ORDER)
    sums = (inner_sums, stream_sums, head_grads)
    lanes = head_grads.shape[-1]
    small = [dealt(x, axes, F32) for x, axes in zip(sums[:2], axes_of)]
    small.append(head_grads.reshape(shape_of(ORDER) + (-1, lanes)).astype(BF16))
    plan = [
        (AllReduce, n + i, n + i, ((axes,), {}), AllReduce.scratch(axes, x.shape[3:], x.dtype))
        for i, (x, axes) in enumerate(zip(small, axes_of))
    ]
    plan += [(Reduce, i, i, ((DP,), {}), Reduce.scratch(DP, block, BF16)) for i in range(n)]
    bulk = tuple(range(3, 3 + n))
    got = exchange(
        cid, lambda: along("t", "f", "row", "col"), plan,
        [g.reshape(sizes + block) for g in grads] + small,
        [like(block, F32)] * n + [like(x.shape, x.dtype) for x in small], [VMEM] * (n + 3),
        order=(0, 1, 2) * 3 + bulk + (0, 1, 2) + bulk * 2, through=through,
    )
    return got[:n], [x.reshape(-1)[: y.size].reshape(y.shape).astype(F32) for x, y in zip(got[n:-1], sums)], got[-1]


def on_device(
    stream,
    scale_first,
    branch_weight,
    branch_bias,
    mixer_weight,
    mixer_bias,
    conv_weight,
    conv_bias,
    decay_weight,
    decay_bias,
    input_weight,
    input_bias,
    decay_param,
    output_weight,
    output_bias,
    scale_second,
    gate_weight,
    gate_bias,
    up_weight,
    up_bias,
    down_weight,
    down_bias,
    cotangent,
):
    mixer_t, branch_t, output_t, stream_all, scale_all, down_pieces = fetch_first(
        mixer_weight.T, branch_weight.T, output_weight.T, stream, scale_first, down_weight.T
    )
    inner = mixer_t.shape[0]
    stream_wide = stream.astype(F32)
    tokens_wide = stream_all.astype(F32)
    inverse_all = lax.rsqrt(jnp.sum(tokens_wide * tokens_wide, axis=1, keepdims=True) / D + EPSILON)
    normed_first = (tokens_wide * inverse_all * (1.0 + scale_all)).astype(BF16)
    mixer_pre = dot_nt(normed_first, mixer_t) + mixer_bias
    branch_pre = dot_nt(normed_first, branch_t) + branch_bias
    branch_act, branch_back = jax.vjp(gelu_tanh, branch_pre)

    steps = mixer_pre.shape[0]
    first_token = lax.axis_index(ORDER) * steps
    position = (first_token + jnp.arange(steps, dtype=jnp.int32)) % LEN
    margin = CONV - 1
    left_edge = from_behind(mixer_pre[steps - margin :], ORDER, 1)
    padded = jnp.concatenate([left_edge, mixer_pre], axis=0)
    conv_out = conv_bias + jnp.zeros_like(mixer_pre)
    for offset in range(CONV):
        in_reach = (position >= offset)[:, None]
        conv_out = conv_out + jnp.where(
            in_reach, conv_weight[offset] * padded[margin - offset : margin - offset + steps], 0.0
        )
    conv_low = conv_out.astype(BF16)
    conv_wide = conv_low.astype(F32)
    heads, block = decay_weight.shape[0], decay_weight.shape[1]
    parts = [conv_low[:, h * block : (h + 1) * block] for h in range(heads)]
    decay_pre = jnp.concatenate([dot_nn(x, decay_weight[h]) for h, x in enumerate(parts)], 1) + decay_bias
    input_pre = jnp.concatenate([dot_nn(x, input_weight[h]) for h, x in enumerate(parts)], 1) + input_bias
    starts = (position == 0)[:, None]

    def gate_values(decay_in, input_in, param_in, conv_in):
        return gates_of(decay_in, input_in, param_in, conv_in, starts)

    (retain, source), gate_back = jax.vjp(gate_values, decay_pre, input_pre, decay_param, conv_wide)
    ones_row = jnp.ones((1, inner), F32)
    states, state_in = recurrence(retain, source, ones_row, False, 3)
    mixed_low = (states * branch_act).astype(BF16)
    first_out = stream_wide + to_stream(dot_nt(mixed_low, output_t).astype(BF16), 4) + output_bias
    second_total, first_total = pair_sum(
        [jnp.sum(x * x, axis=1, keepdims=True) for x in (first_out, stream_wide)], 5
    )
    inverse_second = lax.rsqrt(second_total / D + EPSILON)
    inverse_first = lax.rsqrt(first_total / D + EPSILON)
    normed_second = first_out * inverse_second * (1.0 + scale_second)

    share = down_weight.shape[0] // (2 * TEAM)
    second_all, cot_all, gate_t, up_t, down_t, gate_pre, up_pre = fetch_second(
        normed_second.astype(BF16), cotangent, gate_weight.T, up_weight.T, down_pieces
    )
    mine = (lax.axis_index("t") * 2 + lax.axis_index("col")) * share
    gate_b = lax.dynamic_slice(gate_bias, (mine,), (share,))
    up_b = lax.dynamic_slice(up_bias, (mine,), (share,))

    gate_pre = gate_pre + gate_b
    up_pre = up_pre + up_b
    hidden, hidden_back = jax.vjp(lambda g, u: gelu_tanh(g) * u, gate_pre, up_pre)
    hidden_low = hidden.astype(BF16)
    delta_hidden = dot_nn(cot_all, down_t)
    delta_gate, delta_up = hidden_back(delta_hidden)
    gate_low, up_low = delta_gate.astype(BF16), delta_up.astype(BF16)
    down_part = dot_nt(hidden_low, down_t).astype(BF16)
    down_rows = lax.psum_scatter(down_part, "col", scatter_dimension=1, tiled=True)
    delta_second, grad_gate, grad_up, grad_down = send_second(
        gate_low, up_low, hidden_low, gate_t, up_t, second_all, cot_all, down_part
    )
    delta_result = cotangent.astype(F32)

    norm_second_part, grad_scale_second = normalize_back(
        delta_second, first_out, inverse_second, scale_second, 6
    )
    delta_first = delta_result + norm_second_part
    out_all, mixed_rows, down_rows = to_tokens(delta_first.astype(BF16), mixed_low, down_rows, 7)
    down_proj = lax.psum_scatter(down_rows, ("t", "row"), scatter_dimension=0, tiled=True)
    output_part = dot_tn(core_rows(out_all, 9), mixed_rows).astype(BF16)
    grad_output = lax.psum_scatter(output_part, DP, scatter_dimension=0, tiled=True)
    delta_mixed = dot_nn(out_all, output_t)
    delta_state = delta_mixed * branch_act
    (delta_branch,) = branch_back(delta_mixed * states)
    branch_low = delta_branch.astype(BF16)
    retain_next = jnp.concatenate([retain[1:], ones_row], axis=0)
    back_state, _ = recurrence(retain_next, delta_state, retain[:1], True, 8)
    state_prev = jnp.concatenate([state_in[None], states[:-1]], axis=0)
    delta_decay_pre, delta_input_pre, grad_decay_param, delta_conv = gate_back(
        (back_state * state_prev, back_state)
    )
    decay_low = delta_decay_pre.astype(BF16)
    input_low = delta_input_pre.astype(BF16)

    def split(x):
        return [x[:, h * block : (h + 1) * block] for h in range(heads)]

    grad_decay_weight = jnp.stack([dot_tn(a, b) for a, b in zip(parts, split(decay_low))])
    grad_input_weight = jnp.stack([dot_tn(a, b) for a, b in zip(parts, split(input_low))])
    delta_conv = delta_conv + jnp.concatenate(
        [dot_nt(a, decay_weight[h]) for h, a in enumerate(split(decay_low))], 1
    )
    delta_conv = delta_conv + jnp.concatenate(
        [dot_nt(a, input_weight[h]) for h, a in enumerate(split(input_low))], 1
    )
    delta_padded = jnp.zeros_like(padded)
    conv_grads = []
    for offset in range(CONV):
        in_reach = (position >= offset)[:, None]
        masked = jnp.where(in_reach, delta_conv, 0.0)
        conv_grads.append(
            jnp.sum(masked * padded[margin - offset : margin - offset + steps], axis=0)
        )
        delta_padded = delta_padded + jnp.pad(
            masked * conv_weight[offset], ((margin - offset, offset), (0, 0))
        )
    grad_conv_weight = jnp.stack(conv_grads, axis=0)
    right_edge = from_behind(delta_padded[:margin], ORDER, -1)
    delta_mixer = delta_padded[margin:] + jnp.pad(right_edge, ((steps - margin, 0), (0, 0)))
    mixer_low = delta_mixer.astype(BF16)

    def spread(x):
        return lax.dynamic_update_slice(jnp.zeros_like(gate_bias), x, (mine,))

    small = [
        jnp.sum(delta_branch, axis=0),
        jnp.sum(delta_mixer, axis=0),
        jnp.sum(delta_conv, axis=0),
        jnp.sum(delta_decay_pre, axis=0),
        jnp.sum(delta_input_pre, axis=0),
        grad_decay_param,
        spread(jnp.sum(delta_gate, axis=0)),
        spread(jnp.sum(delta_up, axis=0)),
        grad_conv_weight.reshape(-1),
    ]
    delta_normed_part = dot_nn(branch_low, branch_t) + dot_nn(mixer_low, mixer_t)
    delta_normed_first, first_rows, branch_rows, mixer_rows = finish_block(
        normed_first, branch_low, mixer_low, delta_normed_part.astype(BF16), 10
    )
    norm_first_part, grad_scale_first = normalize_back(
        delta_normed_first, stream_wide, inverse_first, scale_first, 12
    )
    (grad_mixer, grad_branch), (total, stream_sums, head_grads), down_proj = send_first(
        [dot_tn(mixer_rows, first_rows).astype(BF16), dot_tn(branch_rows, first_rows).astype(BF16)],
        jnp.concatenate(small),
        jnp.stack([grad_decay_weight, grad_input_weight]),
        jnp.stack(
            [grad_scale_second, jnp.sum(delta_first, axis=0), jnp.sum(delta_result, axis=0), grad_scale_first]
        ),
        down_proj,
        13,
    )
    result = (first_out + down_proj.astype(F32) + down_bias).astype(BF16)
    grad_stream = delta_first + norm_first_part
    sums, at = [], 0
    for x in small:
        sums.append(total[at : at + x.shape[0]])
        at += x.shape[0]
    return (
        result,
        grad_stream,
        stream_sums[3],
        grad_branch.T,
        sums[0],
        grad_mixer.T,
        sums[1],
        sums[8].reshape(CONV, inner),
        sums[2],
        head_grads[0],
        sums[3],
        head_grads[1],
        sums[4],
        sums[5],
        grad_output.T.astype(F32),
        stream_sums[1],
        stream_sums[0],
        grad_gate.T.astype(F32),
        sums[6],
        grad_up.T.astype(F32),
        sums[7],
        grad_down.astype(F32),
        stream_sums[2],
    )


def solution(mesh):
    shape = mesh.devices.shape
    names = mesh.axis_names
    fleet = mesh.shape["dp"] // TEAM
    at = names.index("dp")
    split_mesh = Mesh(
        mesh.devices.reshape(shape[:at] + (TEAM, fleet) + shape[at + 1 :]),
        names[:at] + DP + names[at + 1 :],
    )
    tokens, fan_in = P((*DP, "row"), "col"), P("col", ("row", *DP))
    fan_out, inner, wide = P("row", ("col", *DP)), P("row"), P("col")
    heads = P("row", None, None)
    return jax.shard_map(
        on_device,
        mesh=split_mesh,
        in_specs=(
            tokens, wide, fan_in, inner, fan_in, inner, P(None, "row"), inner,
            heads, inner, heads, inner, inner, fan_out, wide, wide,
            fan_in, inner, fan_in, inner, fan_out, wide, tokens,
        ),
        out_specs=(
            tokens, tokens, wide, fan_in, inner, fan_in, inner, P(None, "row"), inner,
            heads, inner, heads, inner, inner, fan_out, wide, wide,
            fan_in, inner, fan_in, inner, fan_out, wide,
        ),
        check_vma=False,
    )
```

profile of v0, /device:TPU:0, one launch (start us, length us, event | category | flops | bytes accessed | tf_op | source)
XLA Modules:
  0.0 852.4 jit_solution(16624993446902098919)
XLA Ops:
  7.2 1.3 broadcast_in_dim.126.refs_4_
  8.5 133.3 %shard_map.398 = (bf16[4,2,160,2560]{3,2,1,0:T(8,128)(2,1)}, bf16[4,2,160,2560]{3,2,1,0:T(8,128)(2,1)}, bf16[2,4,2,160,1280]{4,3,2,1,0:T(8,128)(2,1)}, bf16[1,25...) custom-call(bf16[160,1280]{1,0:T(8,128)(2,1)} %bitcast.222, ...), custom_call_target="tpu_custom_call" | custom-call | tf_op jit(solution)/shard_map/pallas_call | solution.py:624
  142.7 1.7 fusion.9
  144.4 4.8 convolution_add_fusion.2
  149.2 2.5 collective-permute-start
  153.6 1.3 add_convert_fusion.1
  157.2 3.1 convert_multiply_fusion.6
  161.0 14.2 %states.1 = (f32[256,1280]{1,0:T(8,128)}, f32[8,1280]{1,0:T(8,128)}) custom-call(f32[256,1280]{1,0:T(8,128)} %get-tuple-element.133.r_ref, f32[256,1280]{1,0:T(8,128)} %get-tuple-element.132.s_ref, f32[8,1280]{1,0:T(8,128)} %broadcast_in_dim_broadcast_in_dim.3.lead_ref), custom_call_target="tpu_custom_call" | custom-call | tf_op jit(solution)/shard_map/states/pallas_call | solution.py:785
  175.1 6.4 multiply_convert_fusion.3
  181.5 5.0 convolution_convert_fusion.4
  186.6 1.2 maximum_bitcast_fusion.refs_0_
  187.8 13.3 %shard_map.399 = f32[256,1280]{1,0:T(8,128)} custom-call(bf16[2,1,256,1280]{3,2,1,0:T(8,128)(2,1)} %maximum_bitcast_fusion.refs_0_), custom_call_target="tpu_custom_call" | custom-call | tf_op jit(solution)/shard_map/pallas_call | solution.py:624
  201.1 1.7 multiply_reduce_fusion.8
  203.9 9.5 %shard_map.400 = f32[2,256,128]{2,1,0:T(8,128)} custom-call(f32[256,128]{1,0:T(8,128)} %pad_maximum_fusion.7.refs_0_), custom_call_target="tpu_custom_call" | custom-call | tf_op jit(solution)/shard_map/pallas_call | solution.py:624
  213.4 1.0 add_bitcast_fusion.2
  215.2 1.0 multiply_convert_fusion.2.n_ref
  216.3 129.0 %fetch_second.1 = (bf16[4,2,256,2560]{3,2,1,0:T(8,128)(2,1)}, bf16[4,2,256,2560]{3,2,1,0:T(8,128)(2,1)}, bf16[1,480,2560]{2,1,0:T(8,128)(2,1)}, bf16[1,480,2560]...) custom-call(bf16[256,1280]{1,0:T(8,128)(2,1)} %multiply_convert_fusion.2.n_ref,, ...), custom_call_target="tpu_custom_call" | custom-call | tf_op jit(solution)/shard_map/fetch_second/pallas_call | solution.py:933
  345.3 16.4 %fusion.169 = (f32[480]{0:T(512)}, bf16[2048,480]{1,0:T(8,128)(2,1)}, bf16[2048,480]{1,0:T(8,128)(2,1)S(1)}, f32[480]{0:T(512)}, bf16[2048,480]{1,0:T(8,128)(2,1)}) fusion(f32[2048,480]{1,0:T(8,128)} %get-tuple-element.66, f32[480]{0:T(512)S(1)} %dynamic_slice.7, f32[2048,480]{1,0:T(8,128)} %get-tuple-element.65, f32[480]{0:T(512)S(1)} %dynamic_slice.6, ...), kind=kOutput, calls=%fused_computation.320 | convolution fusion | flops 5062654976 | bytes 26713600 | tf_op jit(solution)/shard_map/dot_general | solution.py:24
  361.7 1.3 copy-done.32
  363.0 8.3 convolution_convert_fusion.refs_7_
  373.1 1.2 pad_maximum_fusion.1.refs_1_
  374.3 121.2 %send_second.1 = (f32[256,1280]{1,0:T(8,128)}, bf16[480,1280]{1,0:T(8,128)(2,1)}, bf16[480,1280]{1,0:T(8,128)(2,1)}, bf16[4,2,160,480]{3,2,1,0:T(8,128)(2,1)}) custom-call(bf16[2048,480]{1,0:T(8,128)(2,1)} %get-tuple-element.111.refs_0_, bf16[2048,480]{1,0:T(8,128)(2,1)} %get-tuple-element.122.refs_1_, bf16[2048,480]{1,0:T(8,128)(2,1)} %copy-done.32, ...), custom_call_target="tpu_custom_call" | custom-call | tf_op jit(solution)/shard_map/send_second/pallas_call | solution.py:1075
  495.5 2.2 multiply_reduce_fusion.1
  498.5 3.0 shard_map.401
  501.5 1.0 add_bitcast_fusion.1
  503.2 1.0 copy-done.8
  505.2 18.3 %shard_map.402 = (bf16[1,256,2560]{2,1,0:T(8,128)(2,1)}, bf16[2,256,1280]{2,1,0:T(8,128)(2,1)}, bf16[2048,1280]{1,0:T(8,128)(2,1)}) custom-call(bf16[256,1280]{1,0:T(8,128)(2,1)} %convert_element_type.152.refs_0_, bf16[256,1280]{1,0:T(8,128)(2,1)} %copy-done.40, ...), custom_call_target="tpu_custom_call", output_to_operand_aliasing={{2}: (2, {})} | custom-call | tf_op jit(solution)/shard_map/pallas_call | solution.py:624
  523.4 1.4 slice_bitcast_fusion.5
  524.8 1.2 pad_maximum_fusion.4.refs_0_
  526.0 5.6 shard_map.406
  531.6 1.3 broadcast_select_fusion.1
  533.1 3.6 convolution_convert_fusion.1
  538.1 1.1 concatenate.37.r_ref
  542.3 3.0 copy.93
  545.3 4.0 reshape.253
  549.9 3.0 convert_bitcast_fusion.3
  552.9 1.6 convert_bitcast_fusion.2
  555.5 6.8 fusion.174
  562.9 22.4 %back_states.1 = (f32[256,1280]{1,0:T(8,128)}, f32[8,1280]{1,0:T(8,128)}) custom-call(f32[256,1280]{1,0:T(8,128)} %concatenate.37.r_ref, f32[256,1280]{1,0:T(8,128)} %get-tuple-element.125.s_ref, f32[8,1280]{1,0:T(8,128)} %broadcast_in_dim.134.lead_ref), custom_call_target="tpu_custom_call" | custom-call | tf_op jit(solution)/shard_map/back_states/pallas_call | solution.py:785
  585.4 5.4 multiply_reduce_fusion.6
  591.9 1.0 copy-done.33
  595.2 1.0 copy-done.34
  597.0 6.3 multiply_reduce_fusion.4
  603.9 1.7 collective-permute-start.1
  608.0 1.2 pad_maximum_fusion.3
  609.2 1.5 pad_add_fusion
  610.7 3.3 fusion.181
  615.6 5.5 fusion.6
  621.2 1.2 maximum_bitcast_fusion.1.refs_0_
  622.4 22.2 %shard_map.403 = (f32[256,1280]{1,0:T(8,128)}, bf16[256,1280]{1,0:T(8,128)(2,1)}, bf16[2,256,1280]{2,1,0:T(8,128)(2,1)}, bf16[2,256,1280]{2,1,0:T(8,128)(2,1)}) custom-call(bf16[2,1,256,1280]{3,2,1,0:T(8,128)(2,1)} %maximum_bitcast_fusion.1.refs_0_, bf16[2,256,1280]{2,1,0:T(8,128)(2,1)} %pad_maximum_fusion.1.refs_1_, ...), custom_call_target="tpu_custom_call" | custom-call | tf_op jit(solution)/shard_map/pallas_call | solution.py:624
  644.6 1.8 fusion.32
  647.3 10.8 %shard_map.405 = f32[2,256,128]{2,1,0:T(8,128)} custom-call(f32[256,128]{1,0:T(8,128)} %broadcast_in_dim.135.refs_0_), custom_call_target="tpu_custom_call" | custom-call | tf_op jit(solution)/shard_map/pallas_call | solution.py:624
  658.7 1.0 add_bitcast_fusion
  659.9 1.3 broadcast_select_fusion.4
  661.4 3.6 convolution_convert_fusion.3
  665.0 3.7 convolution_convert_fusion.2
  668.7 1.5 fusion.31
  670.2 2.0 convert_bitcast_fusion.4
  672.1 53.3 %reduce-scatter.6.cloned.1.call-done.refs_5_ = bf16[256,1280]{1,0:T(8,128)(2,1)} async-done(((bf16[2048,1280]{1,0:T(8,128)(2,1)}), bf16[256,1280]{1,0:T(8,128)(2,1)}) %reduce-scatter.6.cloned.1.call-update) | async-done | bytes 655376 | tf_op jit(solution)/shard_map/reduce_scatter | solution.py:1286
  725.5 109.7 %shard_map.404 = (f32[160,1280]{1,0:T(8,128)}, f32[160,1280]{1,0:T(8,128)}, f32[4,2,2,8,256]{4,3,2,1,0:T(8,128)}, f32[4,2,2,8,128]{4,3,2,1,0:T(8,128)}, bf16[4,2...) custom-call(bf16[4,2,160,1280]{3,2,1,0:T(8,128)(2,1)} %bitcast.205, ...), custom_call_target="tpu_custom_call", output_to_operand_aliasing={{5}: (5, {})} | custom-call | tf_op jit(solution)/shard_map/pallas_call | solution.py:624
  835.2 1.0 copy.115
  837.4 1.4 fusion.180
  839.5 3.1 fusion.177
  842.6 1.0 add_convert_fusion
  (289 shorter events, 32.4 us)
Async XLA Ops:
  7.2 498.0 %reduce-scatter.4.cloned.1.call-start = ((), (), s32[]{:S(2)}) async-start(), calls=%async_computation.3 | async-start | bytes 15728640 | tf_op jit(solution)/shard_map/reduce_scatter | solution.py:1275
  141.8 2.5 copy-start.18
  141.8 2.5 copy-start.85
  144.4 7.5 copy-start.59
  144.4 7.5 copy-start.52
  144.4 7.6 copy-start.66
  144.4 9.2 %copy-start.63 = (f32[1280]{0:T(1024)S(1)}, f32[1280]{0:T(1024)}, u32[]{:S(2)}) copy-start(f32[1280]{0:T(1024)} %param.30) | copy-start | bytes 15364
  149.2 5.9 copy-start.14
  149.2 5.6 copy-start.25
  149.2 4.3 collective-permute-start
  151.8 3.3 copy-start.67
  151.8 3.3 copy-start.69
  151.8 3.3 copy-start.71
  151.8 5.3 copy-start.75
  151.9 3.2 copy-start.46
  151.9 3.2 copy-start.48
  152.0 3.3 copy-start.73
  154.9 2.3 copy-start.4
  156.2 4.1 copy-start.6
  157.2 3.2 copy-start.2
  161.0 14.2 %copy-start.86 = (f32[1280]{0:T(1024)S(1)}, f32[1280]{0:T(1024)}, u32[]{:S(2)}) copy-start(f32[1280]{0:T(1024)} %param.26) | copy-start | bytes 15364
  181.5 5.0 copy-start.40
  187.8 13.3 %copy-start.12 = (bf16[256,1280]{1,0:T(8,128)(2,1)S(1)}, bf16[256,1280]{1,0:T(8,128)(2,1)}, u32[]{:S(2)}) copy-start(bf16[256,1280]{1,0:T(8,128)(2,1)} %refs_3_.1) | copy-start | bytes 1966084
  187.8 13.3 %copy-start.64 = (f32[1280]{0:T(1024)S(1)}, f32[1280]{0:T(1024)}, u32[]{:S(2)}) copy-start(f32[1280]{0:T(1024)} %param.37) | copy-start | bytes 15364
  202.8 13.4 %copy-start = (f32[256,1280]{1,0:T(8,128)}, f32[256,1280]{1,0:T(8,128)S(1)}, u32[]{:S(2)}) copy-start(f32[256,1280]{1,0:T(8,128)S(1)} %get-tuple-element.119) | copy-start | bytes 3932164
  215.2 130.1 %copy-start.60 = (f32[256]{0:T(256)}, f32[256]{0:T(256)S(1)}, u32[]{:S(2)}) copy-start(f32[256]{0:T(256)S(1)} %get-tuple-element.103) | copy-start | bytes 3076
  345.3 17.7 %copy-start.81 = (bf16[2,4,2,160,480]{4,3,2,1,0:T(8,128)(2,1)S(1)}, bf16[2,4,2,160,480]{4,3,2,1,0:T(8,128)(2,1)}, u32[]{:S(2)}) copy-start(bf16[2,4,2,160,480]{4,3,2,1,0:T(8,128)(2,1)} %get-tuple-element.64) | copy-start | bytes 7372804
  371.3 298.9 %reduce-scatter.8.cloned.1.call-start = ((), (), s32[]{:S(2)}) async-start(), calls=%async_computation.5 | async-start | bytes 3686400 | tf_op jit(solution)/shard_map/reduce_scatter | solution.py:1288
  495.4 7.2 copy-start.1
  495.5 7.2 copy-start.17
  495.5 7.2 copy-start.22
  495.5 7.2 copy-start.61
  495.5 7.2 copy-start.78
  526.0 5.6 copy-start.19
  536.7 188.8 %reduce-scatter.6.cloned.1.call-start = ((), (), s32[]{:S(2)}) async-start(), calls=%async_computation.4 | async-start | bytes 5898240 | tf_op jit(solution)/shard_map/reduce_scatter | solution.py:1286
  538.1 3.7 copy-start.35
  545.3 4.0 copy-start.80
  545.3 4.3 copy-start.79
  549.8 3.1 copy-start.37
  549.8 4.7 copy-start.87
  552.9 2.6 copy-start.36
  562.9 22.5 %copy-start.3 = (f32[256,1280]{1,0:T(8,128)S(1)}, f32[256,1280]{1,0:T(8,128)}, u32[]{:S(2)}) copy-start(f32[256,1280]{1,0:T(8,128)} %copy-done.2) | copy-start | bytes 3932164
  562.9 22.5 %copy-start.5 = (bf16[256,1280]{1,0:T(8,128)(2,1)S(1)}, bf16[256,1280]{1,0:T(8,128)(2,1)}, u32[]{:S(2)}) copy-start(bf16[256,1280]{1,0:T(8,128)(2,1)} %copy-done.4) | copy-start | bytes 1966084
  562.9 22.5 %copy-start.51 = (f32[1280]{0:T(1024)S(1)}, f32[1280]{0:T(1024)}, u32[]{:S(2)}) copy-start(f32[1280]{0:T(1024)} %param.34) | copy-start | bytes 15364
  562.9 22.5 %copy-start.76 = (pred[256]{0:T(512)(128)(4,1)S(1)}, pred[256]{0:T(512)(128)(4,1)}, u32[]{:S(2)}) copy-start(pred[256]{0:T(512)(128)(4,1)} %copy-done.75) | copy-start | bytes 772
  585.4 5.4 copy-start.26
  597.0 6.3 copy-start.47
  597.0 6.3 copy-start.49
  603.8 2.1 copy-start.24
  603.8 6.9 slice-start
  603.9 10.2 %collective-permute-start.1 = (f32[3,1280]{1,0:T(4,128)S(1)}, f32[3,1280]{1,0:T(4,128)S(1)}, u32[]{:S(2)}, u32[]{:S(2)}) collective-permute-start(f32[3,1280]{1,0:T(4,128)S(1)} %pad_add_fusion.1), channel_id=1, source_target_pairs={{1,0},{4,1},{5,4},{8,5},{9,8},{12,9},{13,12},{16,13},{17,16},{20,1... | collective-permute-start | bytes 46088 | tf_op jit(solution)/shard_map/ppermute | solution.py:807
  607.5 3.2 slice-start.1
  610.7 3.4 copy-start.45
  610.7 3.4 copy-start.15
  614.3 6.8 copy-start.29
  622.4 22.2 %copy-start.13 = (bf16[256,1280]{1,0:T(8,128)(2,1)S(1)}, bf16[256,1280]{1,0:T(8,128)(2,1)}, u32[]{:S(2)}) copy-start(bf16[256,1280]{1,0:T(8,128)(2,1)} %refs_3_.1) | copy-start | bytes 1966084
  622.4 22.2 %copy-start.62 = (f32[256]{0:T(256)S(1)}, f32[256]{0:T(256)}, u32[]{:S(2)}) copy-start(f32[256]{0:T(256)} %get-tuple-element.102) | copy-start | bytes 3076
  644.6 15.2 %copy-start.11 = (bf16[256,2560]{1,0:T(8,128)(2,1)S(1)}, bf16[256,2560]{1,0:T(8,128)(2,1)}, u32[]{:S(2)}) copy-start(bf16[256,2560]{1,0:T(8,128)(2,1)} %copy-done.10) | copy-start | bytes 3932164
  661.4 3.6 copy-start.82
  665.0 3.7 copy-start.9
  665.0 3.7 copy-start.16
  665.0 3.7 copy-start.77
  839.5 3.1 copy-start.21
  839.5 3.1 copy-start.65
  (31 other events, 37.4 us)
Sparse Core Ops, SparseCore 0:
  371.4 16.5 reduce-scatter.3
  536.8 84.3 reduce-scatter.7
  624.8 100.6 reduce-scatter.5
where the time goes:
time: 862 us; the launch traced here: 852 us
  Pallas kernels  612 us (71%)
  matrix products  73.6 us (9%)
  waiting for transfers between devices  53.4 us (6%)
  other arithmetic  52.6 us (6%)
  local copies, waits for them, and re-layouts  40.1 us (5%)
  between operations  15.5 us (2%)
    pallas_call x9, Pallas kernels, exchange(): pl.pallas_call(kernel, out_shape=tuple(out_shapes), in_specs=in_specs, ou...  326 us
    pallas_call x1, Pallas kernels, fetch_second(): pl.pallas_call(kernel, out_shape=(every, every, weight, weight, like(down...  129 us
    pallas_call x1, Pallas kernels, send_second(): pl.pallas_call(kernel, out_shape=(like(block, F32), like(weight, BF16), l...  121 us
    reduce_scatter x1, waiting for transfers between devices, on_device(): lax.psum_scatter(down_rows, ('t', 'row'), scatter_dimension=0, tiled=True)  53.3 us
    pallas_call x2, Pallas kernels, recurrence(): pl.pallas_call(kernel, out_shape=(like((rows, width), F32), like((8, widt...  36.6 us
    dot_general x14, matrix products, dot_nn(): return jnp.dot(a, b, preferred_element_type=F32)  33.8 us
    dot_general x14, matrix products, dot_nt(): return lax.dot_general(a, b, NT, preferred_element_type=F32)  26.6 us
  transfers between devices with their start and end apart: 5, of which 1 were waited for; matrix products, arithmetic and copies ran while one was open for 9% of the time, Pallas kernels for 21%

commit v1 on v0

--- a/solution.py
+++ b/solution.py
@@ -337,6 +337,27 @@
             peer = {self.axes[last]: peer_of(self.axes[last], tag[last])}
             self.arrive(self.slot(tag), self.send.at[tag], self.recv.at[tag], peer)
             self.spread(tag)
+
+
+class Widen(Copies):
+    def __init__(self, src, out, scratch):
+        super().__init__()
+        self.src, self.out = src, out
+
+    def begin(self):
+        pass
+
+    def stage(self, wave):
+        if wave == 1:
+            sum_into(self.out, [self.src])
+
+
+class Join(Widen):
+    def stage(self, wave):
+        if wave == 1:
+            share = self.src.shape[-1]
+            for i in range(2 * TEAM):
+                self.out[:, i * share : (i + 1) * share] = self.src[i // 2, i % 2].astype(self.out.dtype)
 
 
 class Fan(Copies):
@@ -1015,17 +1036,11 @@
                 down[n % fleet, n // fleet % TEAM, n // (TEAM * fleet)] = value[j * shard : (j + 1) * shard]
             return carry
 
-        fetch(cot_ref, 0).start()
-        turn(h_ref, ht_ref)
-        greet(team_peers())
-        lax.fori_loop(0, wide // tile, down_gradients, 0)
-        d_job.begin()
-        before = None
-        for tag in sums.order(2):
+        def block_of(tag):
             coords = sums.coords(tag)
             at = pl.ds(pl.multiple_of((coords[0] * r + coords[1]) * rows, rows), rows)
 
-            def product(j, carry, at=at, coords=coords):
+            def product(j, carry):
                 col = pl.ds(pl.multiple_of(j * lane, lane), lane)
                 value = dot_nn(g_ref[at, :], gw_ref[:, col]) + dot_nn(u_ref[at, :], uw_ref[:, col])
                 src[coords[0], coords[1], :, col] = value.astype(BF16)
@@ -1034,13 +1049,6 @@
             lax.fori_loop(0, wide // lane, product, 0)
             for k in offsets("col"):
                 sums.forward(tag + (k,), place(src, sums.coords(tag + (k,))))
-            if before is not None:
-                sums.step(2, before)
-            before = tag
-        sums.step(2, before)
-        middle = sums.order(1)
-        sums.step(1, middle[0])
-        d_job.stage(1)
 
         def gradients(i, carry):
             @pl.when(i + 1 < wide // tile)
@@ -1055,16 +1063,45 @@
                     out[h, j, :, at] = value[j * units : (j + 1) * units]
             return carry
 
-        turn(g_ref, gt_ref)
-        turn(u_ref, ut_ref)
-        for h in (0, 1):
+        def half_gradients(h):
             first = h * (width // tile)
             lax.fori_loop(first, first + width // tile, gradients, 0)
             g_job.begin((h,))
             u_job.begin((h,))
-            sums.step(1, middle[1 + h])
-        for tag in middle[3:]:
-            sums.step(1, tag)
+
+        away = [tag for tag in sums.order(2) if tag[-1]]
+        home = [tag for tag in sums.order(2) if not tag[-1]]
+        team = sums.order(1)
+        fetch(cot_ref, 0).start()
+        greet(team_peers())
+        block_of(away[0])
+        turn(h_ref, ht_ref)
+        sums.step(2, away[0])
+        lax.fori_loop(0, wide // tile, down_gradients, 0)
+        d_job.begin()
+        block_of(away[1])
+        block_of(home[0])
+        sums.step(2, away[1])
+        block_of(away[2])
+        sums.step(2, home[0])
+        sums.step(1, team[0])
+        turn(g_ref, gt_ref)
+        turn(u_ref, ut_ref)
+        half_gradients(0)
+        sums.step(2, away[2])
+        block_of(away[3])
+        block_of(home[1])
+        sums.step(2, away[3])
+        block_of(home[2])
+        sums.step(2, home[1])
+        sums.step(1, team[1])
+        half_gradients(1)
+        d_job.stage(1)
+        sums.step(2, home[2])
+        block_of(home[3])
+        sums.step(1, team[2])
+        sums.step(2, home[3])
+        sums.step(1, team[3])
         sums.stage(3)
         g_job.stage(1)
         u_job.stage(1)
@@ -1094,7 +1131,6 @@
         ),
         name="send_second",
     )(gate, up, hidden, gate_t, up_t, second_all, cot_all, late)
-    grad_down = grad_down.reshape(2 * TEAM, shard, share).transpose(0, 2, 1).reshape(-1, shard)
     return delta, grad_gate, grad_up, grad_down
 
 
@@ -1109,26 +1145,53 @@
     return out
 
 
-def to_tokens(block, mixed, through, cid):
+class FanSwap(Fan):
+    def __init__(self, src, out, sems, other):
+        super().__init__(src, out, "row", sems[:3])
+        self.send_on, self.recv_on = sems[3:]
+        self.other = other
+
+    @staticmethod
+    def scratch():
+        return Fan.scratch("row") + Swap.scratch()
+
+    def stage(self, wave):
+        super().stage(wave)
+        other, width = 1 - lax.axis_index("col"), self.src.shape[-1]
+        if wave == 1:
+            src = self.out.at[0, :, pl.ds(pl.multiple_of(other * width, width), width)]
+            self.push(src, self.other, self.send_on, self.recv_on, {"col": other})
+        if wave == 2:
+            self.arrive(self.other, self.send_on, self.recv_on, {"col": other})
+
+    def drain(self):
+        super().drain()
+        Copies.drain(self)
+
+
+def to_tokens(block, mixed, cid):
     rows, width = block.shape
-    out, both, through = exchange(
-        cid, lambda: across("row", "col"),
-        [
-            (Fan, 0, 0, (("row",), {}), Fan.scratch("row")),
-            (Gather, 1, 1, ((PAIR,), {}), Gather.scratch(PAIR)),
-        ],
-        [block, mixed], [like((1, rows, 2 * width), BF16), like((2,) + mixed.shape, BF16)], [VMEM] * 2,
-        through=through,
-    )
-    return out[0], both.reshape(-1, mixed.shape[1]), through
-
-
-def core_rows(x, cid):
-    (other,) = exchange(
-        cid, lambda: along("col"), [(Swap, 0, 0, ((), {}), Swap.scratch())], [halves(x)],
-        [like((x.shape[0], x.shape[1] // 2), x.dtype)], [VMEM],
-    )
-    return jnp.concatenate(arrange(half_of(x), other), axis=0)
+    fan, gather = FanSwap.scratch(), Gather.scratch(PAIR)
+
+    def kernel(block_ref, mixed_ref, out_ref, other_ref, both_ref, *sems):
+        greet(across("row", "col"))
+        jobs = [
+            FanSwap(block_ref, out_ref, sems[: len(fan)], other_ref),
+            Gather(mixed_ref, both_ref, PAIR, sems[len(fan) :]),
+        ]
+        run_jobs(jobs, ())
+
+    out, other, both = pl.pallas_call(
+        kernel,
+        out_shape=(like((1, rows, 2 * width), BF16), like(block.shape, BF16), like((2,) + mixed.shape, BF16)),
+        in_specs=[VMEM] * 2,
+        out_specs=(VMEM,) * 3,
+        scratch_shapes=fan + gather,
+        compiler_params=pltpu.CompilerParams(collective_id=cid, has_side_effects=True),
+        name="to_tokens",
+    )(block, mixed)
+    both_rows = jnp.concatenate(arrange(half_of(out[0]), other), axis=0)
+    return out[0], both_rows, both.reshape(-1, mixed.shape[1])
 
 
 def dealt(x, axes, dtype):
@@ -1160,7 +1223,7 @@
     return delta, rows, branch.reshape(-1, branch.shape[2]), mixer.reshape(-1, mixer.shape[2])
 
 
-def send_first(grads, inner_sums, head_grads, stream_sums, through, cid):
+def send_first(grads, inner_sums, head_grads, stream_sums, done, through, cid):
     sizes = shape_of(DP)
     n = len(grads)
     block = (grads[0].shape[0] // (sizes[0] * sizes[1]), grads[0].shape[1])
@@ -1175,13 +1238,17 @@
     ]
     plan += [(Reduce, i, i, ((DP,), {}), Reduce.scratch(DP, block, BF16)) for i in range(n)]
     bulk = tuple(range(3, 3 + n))
+    pieces = done[2].shape
+    wide = [like(done[0].shape, F32), like(done[1].shape, F32), like((pieces[2], 2 * TEAM * pieces[3]), F32)]
+    plan += [(cut, n + 3 + i, n + 3 + i, ((), {}), []) for i, cut in enumerate((Widen, Widen, Join))]
+    rest = tuple(range(3 + n, 6 + n))
     got = exchange(
         cid, lambda: along("t", "f", "row", "col"), plan,
-        [g.reshape(sizes + block) for g in grads] + small,
-        [like(block, F32)] * n + [like(x.shape, x.dtype) for x in small], [VMEM] * (n + 3),
-        order=(0, 1, 2) * 3 + bulk + (0, 1, 2) + bulk * 2, through=through,
-    )
-    return got[:n], [x.reshape(-1)[: y.size].reshape(y.shape).astype(F32) for x, y in zip(got[n:-1], sums)], got[-1]
+        [g.reshape(sizes + block) for g in grads] + small + list(done),
+        [like(block, F32)] * n + [like(x.shape, x.dtype) for x in small] + wide, [VMEM] * (n + 6),
+        order=(0, 1, 2) * 3 + bulk + (0, 1, 2) + rest * 2 + bulk * 2, through=through,
+    )
+    return got[:n], [x.reshape(-1)[: y.size].reshape(y.shape).astype(F32) for x, y in zip(got[n : n + 3], sums)], got[n + 3 : -1], got[-1]
 
 
 def on_device(
@@ -1278,13 +1345,13 @@
     )
     delta_result = cotangent.astype(F32)
 
-    norm_second_part, grad_scale_second = normalize_back(
-        delta_second, first_out, inverse_second, scale_second, 6
-    )
+    norm_second_part, grad_scale_second, down_rows = normalize_back(
+        delta_second, first_out, inverse_second, scale_second, 6, down_rows
+    )
+    down_proj = lax.psum_scatter(down_rows, ("t", "row"), scatter_dimension=0, tiled=True)
     delta_first = delta_result + norm_second_part
-    out_all, mixed_rows, down_rows = to_tokens(delta_first.astype(BF16), mixed_low, down_rows, 7)
-    down_proj = lax.psum_scatter(down_rows, ("t", "row"), scatter_dimension=0, tiled=True)
-    output_part = dot_tn(core_rows(out_all, 9), mixed_rows).astype(BF16)
+    out_all, out_rows, mixed_rows = to_tokens(delta_first.astype(BF16), mixed_low, 7)
+    output_part = dot_tn(out_rows, mixed_rows).astype(BF16)
     grad_output = lax.psum_scatter(output_part, DP, scatter_dimension=0, tiled=True)
     delta_mixed = dot_nn(out_all, output_t)
     delta_state = delta_mixed * branch_act
@@ -1347,13 +1414,14 @@
     norm_first_part, grad_scale_first = normalize_back(
         delta_normed_first, stream_wide, inverse_first, scale_first, 12
     )
-    (grad_mixer, grad_branch), (total, stream_sums, head_grads), down_proj = send_first(
+    (grad_mixer, grad_branch), (total, stream_sums, head_grads), wide_grads, down_proj = send_first(
         [dot_tn(mixer_rows, first_rows).astype(BF16), dot_tn(branch_rows, first_rows).astype(BF16)],
         jnp.concatenate(small),
         jnp.stack([grad_decay_weight, grad_input_weight]),
         jnp.stack(
             [grad_scale_second, jnp.sum(delta_first, axis=0), jnp.sum(delta_result, axis=0), grad_scale_first]
         ),
+        (grad_gate, grad_up, grad_down),
         down_proj,
         13,
     )
@@ -1381,11 +1449,11 @@
         grad_output.T.astype(F32),
         stream_sums[1],
         stream_sums[0],
-        grad_gate.T.astype(F32),
+        wide_grads[0].T,
         sums[6],
-        grad_up.T.astype(F32),
+        wide_grads[1].T,
         sums[7],
-        grad_down.astype(F32),
+        wide_grads[2].T,
         stream_sums[2],
     )
 

time: 862 us -> 857 us (level)
  waiting for transfers between devices: 53.4 us -> 70.8 us
  Pallas kernels: 612 us -> 597 us
    pallas_call x9 -> x7, Pallas kernels: 326 us -> 299 us  [exchange(): pl.pallas_call(kernel, out_shape=tuple(out_shapes), in_specs=in_specs, ou...]
    pallas_call x0 -> x1, Pallas kernels: none -> 21.6 us  [to_tokens(): pl.pallas_call(kernel, out_shape=(like((1, rows, 2 * width), BF16), like(...]
    reduce_scatter x1, waiting for transfers between devices: 53.3 us -> 70.7 us  [on_device(): lax.psum_scatter(down_rows, ('t', 'row'), scatter_dimension=0, tiled=True)]
    pallas_call x1, Pallas kernels: 121 us -> 111 us  [send_second(): pl.pallas_call(kernel, out_shape=(like(block, F32), like(weight, BF16), l...]
    unnamed x190 -> x195, local copies, waits for them, and re-layouts: 13.2 us -> 19.8 us
  transfers between devices with their start and end apart: 5 -> 5, of which waited for: 1 -> 1; matrix products, arithmetic and copies ran while one was open for 9% -> 8% of each run, Pallas kernels for 21% -> 19%
where the time goes in v1:
time: 857 us; the launch traced here: 847 us
  Pallas kernels  597 us (70%)
  matrix products  75.2 us (9%)
  waiting for transfers between devices  70.8 us (8%)
  other arithmetic  46.3 us (5%)
  local copies, waits for them, and re-layouts  37.1 us (4%)
  between operations  15.5 us (2%)
    pallas_call x7, Pallas kernels, exchange(): pl.pallas_call(kernel, out_shape=tuple(out_shapes), in_specs=in_specs, ou...  299 us
    pallas_call x1, Pallas kernels, fetch_second(): pl.pallas_call(kernel, out_shape=(every, every, weight, weight, like(down...  129 us
    pallas_call x1, Pallas kernels, send_second(): pl.pallas_call(kernel, out_shape=(like(block, F32), like(weight, BF16), l...  111 us
    reduce_scatter x1, waiting for transfers between devices, on_device(): lax.psum_scatter(down_rows, ('t', 'row'), scatter_dimension=0, tiled=True)  70.7 us
    pallas_call x2, Pallas kernels, recurrence(): pl.pallas_call(kernel, out_shape=(like((rows, width), F32), like((8, widt...  37.1 us
    dot_general x14, matrix products, dot_nn(): return jnp.dot(a, b, preferred_element_type=F32)  35.5 us
    dot_general x14, matrix products, dot_nt(): return lax.dot_general(a, b, NT, preferred_element_type=F32)  26.6 us
    pallas_call x1, Pallas kernels, to_tokens(): pl.pallas_call(kernel, out_shape=(like((1, rows, 2 * width), BF16), like(...  21.6 us
  transfers between devices with their start and end apart: 5, of which 1 were waited for; matrix products, arithmetic and copies ran while one was open for 8% of the time, Pallas kernels for 19%

profile of v1, /device:TPU:0, one launch (start us, length us, event | category | flops | bytes accessed | tf_op | source)
XLA Modules:
  0.0 847.2 jit_solution(2480492082581552908)
XLA Ops:
  7.2 1.3 broadcast_in_dim.126.refs_4_
  8.5 133.3 %shard_map.398 = (bf16[4,2,160,2560]{3,2,1,0:T(8,128)(2,1)}, bf16[4,2,160,2560]{3,2,1,0:T(8,128)(2,1)}, bf16[2,4,2,160,1280]{4,3,2,1,0:T(8,128)(2,1)}, bf16[1,25...) custom-call(bf16[160,1280]{1,0:T(8,128)(2,1)} %bitcast.212, ...), custom_call_target="tpu_custom_call" | custom-call | tf_op jit(solution)/shard_map/pallas_call | solution.py:645
  142.7 1.7 fusion.9
  144.4 4.8 convolution_add_fusion.2
  149.3 2.5 collective-permute-start
  153.6 1.3 add_convert_fusion.1
  157.2 3.1 convert_multiply_fusion.6
  161.0 14.2 %states.1 = (f32[256,1280]{1,0:T(8,128)}, f32[8,1280]{1,0:T(8,128)}) custom-call(f32[256,1280]{1,0:T(8,128)} %get-tuple-element.143.r_ref, f32[256,1280]{1,0:T(8,128)} %get-tuple-element.142.s_ref, f32[8,1280]{1,0:T(8,128)} %broadcast_in_dim_broadcast_in_dim.3.lead_ref), custom_call_target="tpu_custom_call" | custom-call | tf_op jit(solution)/shard_map/states/pallas_call | solution.py:806
  175.2 6.4 multiply_convert_fusion.3
  181.6 5.0 convolution_convert_fusion.4
  186.7 1.2 maximum_bitcast_fusion.refs_0_
  187.9 13.3 %shard_map.399 = f32[256,1280]{1,0:T(8,128)} custom-call(bf16[2,1,256,1280]{3,2,1,0:T(8,128)(2,1)} %maximum_bitcast_fusion.refs_0_), custom_call_target="tpu_custom_call" | custom-call | tf_op jit(solution)/shard_map/pallas_call | solution.py:645
  201.2 1.7 multiply_reduce_fusion.8
  204.0 9.5 %shard_map.400 = f32[2,256,128]{2,1,0:T(8,128)} custom-call(f32[256,128]{1,0:T(8,128)} %pad_maximum_fusion.6.refs_0_), custom_call_target="tpu_custom_call" | custom-call | tf_op jit(solution)/shard_map/pallas_call | solution.py:645
  213.5 1.0 add_bitcast_fusion.2
  215.3 1.0 multiply_convert_fusion.2.n_ref
  216.3 129.0 %fetch_second.1 = (bf16[4,2,256,2560]{3,2,1,0:T(8,128)(2,1)}, bf16[4,2,256,2560]{3,2,1,0:T(8,128)(2,1)}, bf16[1,480,2560]{2,1,0:T(8,128)(2,1)}, bf16[1,480,2560]...) custom-call(bf16[256,1280]{1,0:T(8,128)(2,1)} %multiply_convert_fusion.2.n_ref,, ...), custom_call_target="tpu_custom_call" | custom-call | tf_op jit(solution)/shard_map/fetch_second/pallas_call | solution.py:954
  345.4 16.4 %fusion.169 = (f32[480]{0:T(512)}, bf16[2048,480]{1,0:T(8,128)(2,1)}, bf16[2048,480]{1,0:T(8,128)(2,1)S(1)}, f32[480]{0:T(512)}, bf16[2048,480]{1,0:T(8,128)(2,1)}) fusion(f32[2048,480]{1,0:T(8,128)} %get-tuple-element.71, f32[480]{0:T(512)S(1)} %dynamic_slice.7, f32[2048,480]{1,0:T(8,128)} %get-tuple-element.70, f32[480]{0:T(512)S(1)} %dynamic_slice.6, ...), kind=kOutput, calls=%fused_computation.314 | convolution fusion | flops 5062654976 | bytes 26713600 | tf_op jit(solution)/shard_map/dot_general | solution.py:24
  361.8 1.3 copy-done.34
  363.1 8.3 convolution_convert_fusion.refs_7_
  371.6 110.7 %send_second.1 = (f32[256,1280]{1,0:T(8,128)}, bf16[480,1280]{1,0:T(8,128)(2,1)}, bf16[480,1280]{1,0:T(8,128)(2,1)}, bf16[4,2,160,480]{3,2,1,0:T(8,128)(2,1)}) custom-call(bf16[2048,480]{1,0:T(8,128)(2,1)} %get-tuple-element.121.refs_0_, bf16[2048,480]{1,0:T(8,128)(2,1)} %get-tuple-element.132.refs_1_, bf16[2048,480]{1,0:T(8,128)(2,1)} %copy-done.34, ...), custom_call_target="tpu_custom_call" | custom-call | tf_op jit(solution)/shard_map/send_second/pallas_call | solution.py:1112
  482.4 2.1 multiply_reduce_fusion.1
  485.2 3.2 shard_map.401
  488.4 1.0 add_bitcast_fusion.1
  490.1 1.0 copy-done.8
  491.2 0.9 convert_element_type.128.block_ref
  492.1 21.6 %to_tokens.1 = (bf16[1,256,2560]{2,1,0:T(8,128)(2,1)}, bf16[256,1280]{1,0:T(8,128)(2,1)}, bf16[2,256,1280]{2,1,0:T(8,128)(2,1)}) custom-call(bf16[256,1280]{1,0:T(8,128)(2,1)} %convert_element_type.128.block_ref, bf16[256,1280]{1,0:T(8,128)(2,1)} %copy-done.39), custom_call_target="tpu_custom_call" | custom-call | tf_op jit(solution)/shard_map/to_tokens/pallas_call | solution.py:1184
  513.7 1.7 broadcast_select_fusion.1
  515.6 3.6 convolution_convert_fusion.1
  521.0 1.0 copy-done.10
  522.0 1.2 pad_maximum_fusion.1.refs_1_
  523.9 1.1 concatenate.37.r_ref
  526.9 8.5 fusion.174
  536.0 22.9 %back_states.1 = (f32[256,1280]{1,0:T(8,128)}, f32[8,1280]{1,0:T(8,128)}) custom-call(f32[256,1280]{1,0:T(8,128)} %concatenate.37.r_ref, f32[256,1280]{1,0:T(8,128)} %get-tuple-element.135.s_ref, f32[8,1280]{1,0:T(8,128)} %broadcast_in_dim.134.lead_ref), custom_call_target="tpu_custom_call" | custom-call | tf_op jit(solution)/shard_map/back_states/pallas_call | solution.py:806
  558.9 5.4 multiply_reduce_fusion.6
  565.5 1.0 copy-done.35
  568.7 1.0 copy-done.36
  570.6 6.1 multiply_reduce_fusion.4
  577.3 1.7 collective-permute-start.1
  581.4 1.2 pad_maximum_fusion.3
  582.6 1.5 pad_add_fusion
  584.1 3.3 fusion.181
  589.0 5.5 fusion.6
  594.6 1.2 maximum_bitcast_fusion.1.refs_0_
  595.8 16.1 %shard_map.402 = (f32[256,1280]{1,0:T(8,128)}, bf16[256,1280]{1,0:T(8,128)(2,1)}, bf16[2,256,1280]{2,1,0:T(8,128)(2,1)}, bf16[2,256,1280]{2,1,0:T(8,128)(2,1)}) custom-call(bf16[2,1,256,1280]{3,2,1,0:T(8,128)(2,1)} %maximum_bitcast_fusion.1.refs_0_, bf16[2,256,1280]{2,1,0:T(8,128)(2,1)} %pad_maximum_fusion.1.refs_1_, ...), custom_call_target="tpu_custom_call" | custom-call | tf_op jit(solution)/shard_map/pallas_call | solution.py:645
  611.9 1.8 fusion.32
  614.5 10.6 %shard_map.404 = f32[2,256,128]{2,1,0:T(8,128)} custom-call(f32[256,128]{1,0:T(8,128)} %broadcast_in_dim.135.refs_0_), custom_call_target="tpu_custom_call" | custom-call | tf_op jit(solution)/shard_map/pallas_call | solution.py:645
  625.7 1.0 add_bitcast_fusion
  626.8 1.3 broadcast_select_fusion.3
  628.4 3.6 convolution_convert_fusion.3
  632.0 3.7 convolution_convert_fusion.2
  635.7 1.5 fusion.31
  637.2 2.0 convert_bitcast_fusion.1
  639.1 70.7 %reduce-scatter.6.cloned.1.call-done.refs_8_ = bf16[256,1280]{1,0:T(8,128)(2,1)} async-done(((bf16[2048,1280]{1,0:T(8,128)(2,1)}), bf16[256,1280]{1,0:T(8,128)(2,1)}) %reduce-scatter.6.cloned.1.call-update) | async-done | bytes 655376 | tf_op jit(solution)/shard_map/reduce_scatter | solution.py:1351
  709.8 113.1 %shard_map.403 = (f32[160,1280]{1,0:T(8,128)}, f32[160,1280]{1,0:T(8,128)}, f32[4,2,2,8,256]{4,3,2,1,0:T(8,128)}, f32[4,2,2,8,128]{4,3,2,1,0:T(8,128)}, bf16[4,2...) custom-call(bf16[4,2,160,1280]{3,2,1,0:T(8,128)(2,1)} %bitcast.191, ...), custom_call_target="tpu_custom_call", output_to_operand_aliasing={{8}: (8, {})} | custom-call | tf_op jit(solution)/shard_map/pallas_call | solution.py:645
  822.9 1.0 copy.113
  825.1 1.4 fusion.180
  827.2 3.1 fusion.177
  830.3 1.0 add_convert_fusion
  833.8 1.4 copy.160
  835.3 1.1 copy-done.32
  836.4 1.4 copy.161
  837.9 1.1 copy-done.31
  839.0 1.4 copy.162
  (286 shorter events, 28.9 us)
Async XLA Ops:
  7.2 477.2 %reduce-scatter.4.cloned.1.call-start = ((), (), s32[]{:S(2)}) async-start(), calls=%async_computation.3 | async-start | bytes 15728640 | tf_op jit(solution)/shard_map/reduce_scatter | solution.py:1342
  141.8 2.6 copy-start.18
  141.8 2.6 copy-start.87
  142.7 32.5 %copy-start.50 = (f32[2560]{0:T(1024)}, f32[2560]{0:T(1024)S(1)}, u32[]{:S(2)}) copy-start(f32[2560]{0:T(1024)S(1)} %add.281) | copy-start | bytes 30724
  144.4 30.8 %copy-start.79 = (f32[256]{0:T(256)}, f32[256]{0:T(256)S(1)}, u32[]{:S(2)}) copy-start(f32[256]{0:T(256)S(1)} %add_rsqrt_fusion) | copy-start | bytes 3076
  144.4 7.5 copy-start.58
  144.4 7.5 copy-start.52
  144.4 7.6 copy-start.65
  144.4 9.2 %copy-start.62 = (f32[1280]{0:T(1024)S(1)}, f32[1280]{0:T(1024)}, u32[]{:S(2)}) copy-start(f32[1280]{0:T(1024)} %param.30) | copy-start | bytes 15364
  149.2 11.1 %copy-start.14 = (f32[256,1280]{1,0:T(8,128)}, f32[256,1280]{1,0:T(8,128)S(1)}, u32[]{:S(2)}) copy-start(f32[256,1280]{1,0:T(8,128)S(1)} %convolution_add_fusion.2) | copy-start | bytes 3932164
  149.3 5.6 copy-start.24
  149.3 4.3 collective-permute-start
  151.8 3.3 copy-start.67
  151.8 3.3 copy-start.69
  151.9 3.3 copy-start.71
  151.9 5.3 copy-start.75
  152.0 3.2 copy-start.44
  152.0 3.2 copy-start.46
  152.0 3.3 copy-start.73
  154.9 2.3 copy-start.4
  156.2 4.1 copy-start.6
  157.2 3.2 copy-start.2
  161.0 14.2 %copy-start.88 = (f32[1280]{0:T(1024)S(1)}, f32[1280]{0:T(1024)}, u32[]{:S(2)}) copy-start(f32[1280]{0:T(1024)} %param.26) | copy-start | bytes 15364
  181.6 5.0 copy-start.39
  187.9 13.3 %copy-start.12 = (bf16[256,1280]{1,0:T(8,128)(2,1)S(1)}, bf16[256,1280]{1,0:T(8,128)(2,1)}, u32[]{:S(2)}) copy-start(bf16[256,1280]{1,0:T(8,128)(2,1)} %refs_3_.1) | copy-start | bytes 1966084
  187.9 13.3 %copy-start.63 = (f32[1280]{0:T(1024)S(1)}, f32[1280]{0:T(1024)}, u32[]{:S(2)}) copy-start(f32[1280]{0:T(1024)} %param.37) | copy-start | bytes 15364
  202.9 13.5 %copy-start = (f32[256,1280]{1,0:T(8,128)}, f32[256,1280]{1,0:T(8,128)S(1)}, u32[]{:S(2)}) copy-start(f32[256,1280]{1,0:T(8,128)S(1)} %get-tuple-element.129) | copy-start | bytes 3932164
  215.3 130.1 %copy-start.59 = (f32[256]{0:T(256)}, f32[256]{0:T(256)S(1)}, u32[]{:S(2)}) copy-start(f32[256]{0:T(256)S(1)} %get-tuple-element.113) | copy-start | bytes 3076
  345.4 17.7 %copy-start.83 = (bf16[2,4,2,160,480]{4,3,2,1,0:T(8,128)(2,1)S(1)}, bf16[2,4,2,160,480]{4,3,2,1,0:T(8,128)(2,1)}, u32[]{:S(2)}) copy-start(bf16[2,4,2,160,480]{4,3,2,1,0:T(8,128)(2,1)} %get-tuple-element.69) | copy-start | bytes 7372804
  371.4 265.8 %reduce-scatter.8.cloned.1.call-start = ((), (), s32[]{:S(2)}) async-start(), calls=%async_computation.5 | async-start | bytes 3686400 | tf_op jit(solution)/shard_map/reduce_scatter | solution.py:1355
  485.2 4.3 copy-start.1
  485.2 4.3 copy-start.17
  485.2 4.3 copy-start.21
  485.2 4.4 copy-start.60
  485.2 4.4 copy-start.78
  519.2 190.6 %reduce-scatter.6.cloned.1.call-start = ((), (), s32[]{:S(2)}) async-start(), calls=%async_computation.4 | async-start | bytes 5898240 | tf_op jit(solution)/shard_map/reduce_scatter | solution.py:1351
  523.8 2.6 copy-start.82
  523.8 2.7 copy-start.81
  536.0 22.9 %copy-start.3 = (f32[256,1280]{1,0:T(8,128)S(1)}, f32[256,1280]{1,0:T(8,128)}, u32[]{:S(2)}) copy-start(f32[256,1280]{1,0:T(8,128)} %copy-done.2) | copy-start | bytes 3932164
  536.0 22.9 %copy-start.5 = (bf16[256,1280]{1,0:T(8,128)(2,1)S(1)}, bf16[256,1280]{1,0:T(8,128)(2,1)}, u32[]{:S(2)}) copy-start(bf16[256,1280]{1,0:T(8,128)(2,1)} %copy-done.4) | copy-start | bytes 1966084
  536.0 22.9 %copy-start.49 = (f32[1280]{0:T(1024)S(1)}, f32[1280]{0:T(1024)}, u32[]{:S(2)}) copy-start(f32[1280]{0:T(1024)} %param.34) | copy-start | bytes 15364
  536.0 23.0 %copy-start.76 = (pred[256]{0:T(512)(128)(4,1)S(1)}, pred[256]{0:T(512)(128)(4,1)}, u32[]{:S(2)}) copy-start(pred[256]{0:T(512)(128)(4,1)} %copy-done.75) | copy-start | bytes 772
  558.9 5.4 copy-start.25
  570.5 6.2 copy-start.45
  570.5 6.2 copy-start.47
  570.5 6.2 copy-start.74
  577.2 6.9 slice-start
  577.3 10.3 %collective-permute-start.1 = (f32[3,1280]{1,0:T(4,128)S(1)}, f32[3,1280]{1,0:T(4,128)S(1)}, u32[]{:S(2)}, u32[]{:S(2)}) collective-permute-start(f32[3,1280]{1,0:T(4,128)S(1)} %pad_add_fusion.1), channel_id=1, source_target_pairs={{1,0},{4,1},{5,4},{8,5},{9,8},{12,9},{13,12},{16,13},{17,16},{20,1... | collective-permute-start | bytes 46088 | tf_op jit(solution)/shard_map/ppermute | solution.py:828
  581.0 3.2 slice-start.1
  584.1 3.4 copy-start.66
  584.1 3.4 copy-start.15
  587.8 6.7 copy-start.28
  595.8 16.1 %copy-start.13 = (bf16[256,1280]{1,0:T(8,128)(2,1)S(1)}, bf16[256,1280]{1,0:T(8,128)(2,1)}, u32[]{:S(2)}) copy-start(bf16[256,1280]{1,0:T(8,128)(2,1)} %refs_3_.1) | copy-start | bytes 1966084
  595.8 16.1 %copy-start.61 = (f32[256]{0:T(256)S(1)}, f32[256]{0:T(256)}, u32[]{:S(2)}) copy-start(f32[256]{0:T(256)} %get-tuple-element.112) | copy-start | bytes 3076
  611.9 14.9 %copy-start.11 = (bf16[256,2560]{1,0:T(8,128)(2,1)S(1)}, bf16[256,2560]{1,0:T(8,128)(2,1)}, u32[]{:S(2)}) copy-start(bf16[256,2560]{1,0:T(8,128)(2,1)} %copy-done.10) | copy-start | bytes 3932164
  628.4 3.6 copy-start.84
  632.0 3.7 copy-start.9
  632.0 3.7 copy-start.16
  632.0 3.7 copy-start.77
  827.2 3.1 copy-start.20
  827.2 3.1 copy-start.64
  831.6 2.3 copy-start.33
  833.8 2.6 copy-start.32
  836.4 2.6 copy-start.31
  (32 other events, 38.6 us)
Sparse Core Ops, SparseCore 0:
  371.5 17.1 reduce-scatter.3
  519.3 84.8 reduce-scatter.7
  607.8 101.9 reduce-scatter.5

commit v2 on v1

--- a/solution.py
+++ b/solution.py
@@ -1,3 +1,5 @@
+import math
+
 import jax
 import jax.numpy as jnp
 from jax import lax
@@ -11,6 +13,7 @@
 LEN = 4096
 EPSILON = 1e-06
 SQRT_FLOOR = 0.0001
+GELU = (2.0 / math.pi) ** 0.5
 TEAM = 4
 NT = (((1,), (1,)), ((), ()))
 TN = (((0,), (0,)), ((), ()))
@@ -524,7 +527,7 @@
         self.each(left)
 
 
-class Trade(Copies):
+class Deal(Copies):
     def __init__(self, src, out, scratch):
         super().__init__()
         self.src, self.out = src, out
@@ -533,28 +536,44 @@
     @staticmethod
     def scratch(piece, dtype):
         shape = shape_of(("t", "col"))
-        sems = [pltpu.SemaphoreType.DMA(shape), pltpu.SemaphoreType.DMA(shape), pltpu.SemaphoreType.DMA]
-        return [pltpu.VMEM(shape + piece, dtype)] + sems
+        sems = pltpu.SemaphoreType.DMA(shape + (lax.axis_size("f"),))
+        return [pltpu.VMEM(shape + piece, dtype), sems, sems, pltpu.SemaphoreType.DMA]
+
+    def onward(self, tag):
+        t, c = source_of("t", tag[0]), source_of("col", tag[1])
+        slot = self.out.at[c, t, lax.axis_index("f")]
+        src = slot if any(tag) else self.cut.at[t, c]
+        for k in offsets("f"):
+            at = tag + (k,)
+            self.push(src, slot, self.send.at[at], self.recv.at[at], {"f": peer_of("f", k)})
 
     def begin(self):
         share = self.cut.shape[-1]
         for i in range(2 * TEAM):
             self.cut[i // 2, i % 2] = self.src[:, i * share : (i + 1) * share]
-        t, c = lax.axis_index("t"), lax.axis_index("col")
+        t, c, f = (lax.axis_index(a) for a in ("t", "col", "f"))
         for tag in grid_of(("t", "col")):
             to = peer_of("t", tag[0]), peer_of("col", tag[1])
             if any(tag):
-                peer = {"t": to[0], "col": to[1]}
-                self.push(self.cut.at[to], self.out.at[c, t], self.send.at[tag], self.recv.at[tag], peer)
-        self.keep(self.cut.at[t, c], self.out.at[c, t], self.own)
+                peer, at = {"t": to[0], "col": to[1]}, tag + (0,)
+                self.push(self.cut.at[to], self.out.at[c, t, f], self.send.at[at], self.recv.at[at], peer)
+        self.onward((0, 0))
+        self.keep(self.cut.at[t, c], self.out.at[c, t, f], self.own)
 
     def stage(self, wave):
-        if wave == 1:
-            for tag in grid_of(("t", "col")):
-                if any(tag):
-                    peer = source_of("t", tag[0]), source_of("col", tag[1])
-                    slot = self.out.at[peer[1], peer[0]]
-                    self.arrive(slot, self.send.at[tag], self.recv.at[tag], {"t": peer[0], "col": peer[1]})
+        f = lax.axis_index("f")
+        for tag in grid_of(("t", "col")):
+            t, c = source_of("t", tag[0]), source_of("col", tag[1])
+            if wave == 1 and any(tag):
+                at = tag + (0,)
+                slot = self.out.at[c, t, f]
+                self.arrive(slot, self.send.at[at], self.recv.at[at], {"t": t, "col": c})
+                self.onward(tag)
+            if wave == 2:
+                for k in offsets("f"):
+                    at = tag + (k,)
+                    slot = self.out.at[c, t, source_of("f", k)]
+                    self.arrive(slot, self.send.at[at], self.recv.at[at], {"f": source_of("f", k)})
 
 
 class Undeal(Copies):
@@ -870,10 +889,11 @@
 PAIR = ("col",)
 
 
-def fetch_first(mixer, branch, output, stream, scale, down):
+def fetch_first(mixer, branch, output, stream, scale, cotangent):
     t, f, c = shape_of(WEIGHT_AXES)
     width, inner = mixer.shape
-    piece = (down.shape[0], down.shape[1] // (2 * TEAM))
+    rows, half = cotangent.shape
+    team, r, _ = shape_of(TOKEN_AXES)
     place = lanes_of(inner)
     axes = (WEIGHT_AXES,)
     plan = [
@@ -882,52 +902,64 @@
         (Gather, 1, 1, (axes, {"place": place}), Gather.scratch(WEIGHT_AXES)),
         (Gather, 2, 2, (axes, {"place": col_first}), Gather.scratch(WEIGHT_AXES)),
         (Gather, 4, 4, ((PAIR,), {}), Gather.scratch(PAIR)),
-        (Trade, 5, 5, ((), {}), Trade.scratch(piece, BF16)),
+        (Gather, 5, 5, ((TOKEN_AXES,), {"place": lanes_of(half)}), Gather.scratch(TOKEN_AXES)),
     ]
     wide = like((t, f, width, 2 * inner), BF16)
     outs = [wide, wide, like((c, t, f) + output.shape, BF16), like((1, stream.shape[0], 2 * stream.shape[1]), BF16)]
-    outs += [like((2, 1, scale.shape[0]), F32), like((2, TEAM) + piece, BF16)]
-    mixer_t, branch_t, output_t, tokens, scale, down = exchange(
-        0, lambda: along("t", "f") + across("row", "col") + diagonal("t", "col"), plan,
-        [mixer, branch, output, stream, scale[None], down], outs, [ANY] * 4 + [VMEM, ANY],
-        order=(0, 1, 2, 3, 4, 0, 5, 2, 3),
-    )
-    return mixer_t.reshape(-1, 2 * inner), branch_t.reshape(-1, 2 * inner), output_t.reshape(-1, output.shape[1]), tokens[0], scale.reshape(-1), down
-
-
-def fetch_second(normed, cotangent, gate, up, down):
+    outs += [like((2, 1, scale.shape[0]), F32), like((team, r, rows, 2 * half), BF16)]
+    mixer_t, branch_t, output_t, tokens, scale, every = exchange(
+        0, lambda: along("t", "f") + across("row", "col"), plan,
+        [mixer, branch, output, stream, scale[None], cotangent], outs, [ANY] * 4 + [VMEM, ANY],
+    )
+    return mixer_t.reshape(-1, 2 * inner), branch_t.reshape(-1, 2 * inner), output_t.reshape(-1, output.shape[1]), tokens[0], scale.reshape(-1), every.reshape(-1, 2 * half)
+
+
+def fetch_second(normed, gate, up, down, gate_bias, up_bias):
     t, r, _ = shape_of(TOKEN_AXES)
     fleet = lax.axis_size("f")
     rows, width = normed.shape
     units, inner = gate.shape
-    share = down.shape[-1]
+    share = down.shape[1] // (2 * TEAM)
+    piece = (down.shape[0], share)
     half = fleet // 2
+    deal = Deal.scratch(piece, BF16)
     token, fan = Gather.scratch(TOKEN_AXES), Fan.scratch("f")
     place = lanes_of(width)
-
-    def kernel(n_ref, c_ref, g_ref, u_ref, d_ref, n_all, c_all, gw, uw, d_all, g_out, u_out, held, sem, *rest):
+    step = next(n for n in (32, 16, 8, rows) if rows % n == 0)
+
+    def kernel(n_ref, g_ref, u_ref, d_ref, gb, ub, n_all, gw, uw, d_all, g_out, u_out, h_out, held, sem, *rest):
         normed_job = Gather(n_ref, n_all, TOKEN_AXES, rest[:3], place)
-        cot_job = Gather(c_ref, c_all, TOKEN_AXES, rest[3:6], place)
-        gate_job, up_job = Fan(g_ref, gw, "f", rest[6:9]), Fan(u_ref, uw, "f", rest[9:12])
-        down_job = Gather(d_ref, d_all, ("f",), rest[12:15], lambda ref, at: ref.at[:, :, at[0]])
-        jobs = (normed_job, gate_job, up_job, down_job, cot_job)
-        greet(along("t", "row") + across("f", "col"))
-        for job in jobs:
+        gate_job, up_job = Fan(g_ref, gw, "f", rest[3:6]), Fan(u_ref, uw, "f", rest[6:9])
+        down_job = Deal(d_ref, d_all, rest[9:])
+        greet(team_peers())
+        for job in (normed_job, gate_job, up_job):
             job.begin()
         normed_job.stage(1)
-        cot_job.stage(1)
+        down_job.begin()
         normed_job.stage(2)
         normed_job.stage(3)
         normed_job.drain()
         for job in (gate_job, up_job):
             job.stage(1)
             job.drain()
+        down_job.stage(1)
         blocks = t * r
 
         def fetch(i):
             return pltpu.make_async_copy(n_all.at[i // r, i % r], held.at[i % 2], sem.at[i % 2])
 
         fetch(0).start()
+
+        def bend(i, carry):
+            at = pl.ds(pl.multiple_of(i * step, step), step)
+            v, u = g_out[at, :] + gb[...], u_out[at, :] + ub[...]
+            bent = jnp.tanh(GELU * (v + 0.044715 * v * v * v))
+            cdf = 0.5 * (1.0 + bent)
+            slope = cdf + 0.5 * v * (1.0 - bent * bent) * (GELU * (1.0 + 3.0 * 0.044715 * v * v))
+            h_out[at, :] = (v * cdf * u).astype(BF16)
+            g_out[at, :] = u * slope
+            u_out[at, :] = v * cdf
+            return carry
 
         def product(i, carry):
             @pl.when(i + 1 < blocks)
@@ -939,36 +971,34 @@
             for weight, out in ((gw, g_out), (uw, u_out)):
                 for j in range(half):
                     out[at, j * units : (j + 1) * units] = dot_nt(held[i % 2], weight[j])
+            lax.fori_loop(i * (rows // step), (i + 1) * (rows // step), bend, 0)
             return carry
 
         lax.fori_loop(0, blocks, product, 0)
-        cot_job.stage(2)
-        down_job.stage(1)
-        cot_job.stage(3)
-        for job in (down_job, cot_job):
-            job.drain()
+        down_job.stage(2)
+        down_job.drain()
 
     every = like((t, r, rows, 2 * width), BF16)
     weight = like((half, units, 2 * inner), BF16)
     first = like((t * r * rows, share), F32)
-    n_all, c_all, gate_t, up_t, down_t, gate_out, up_out = pl.pallas_call(
+    n_all, gate_t, up_t, down_t, gate_slope, up_slope, hidden = pl.pallas_call(
         kernel,
-        out_shape=(every, every, weight, weight, like(down.shape[:2] + (fleet,) + down.shape[2:], BF16), first, first),
-        in_specs=[VMEM] * 5,
-        out_specs=(ANY, ANY, VMEM, VMEM, ANY, VMEM, VMEM),
+        out_shape=(every, weight, weight, like((2, t, fleet) + piece, BF16), first, first, like(first.shape, BF16)),
+        in_specs=[VMEM] * 6,
+        out_specs=(ANY, VMEM, VMEM, ANY, VMEM, VMEM, VMEM),
         scratch_shapes=[pltpu.VMEM((2, rows, 2 * width), BF16), pltpu.SemaphoreType.DMA((2,))]
-        + token + token + fan + fan + Gather.scratch(("f",)),
+        + token + fan + fan + deal,
         compiler_params=pltpu.CompilerParams(collective_id=1, has_side_effects=True),
         name="fetch_second",
-    )(normed, cotangent, gate, up, down)
+    )(normed, gate, up, down, gate_bias[None], up_bias[None])
     return (
         n_all.reshape(-1, 2 * width),
-        c_all.reshape(-1, 2 * width),
         gate_t.reshape(-1, 2 * inner),
         up_t.reshape(-1, 2 * inner),
         down_t.reshape(-1, share),
-        gate_out,
-        up_out,
+        gate_slope,
+        up_slope,
+        hidden,
     )
 
 
@@ -1246,7 +1276,7 @@
         cid, lambda: along("t", "f", "row", "col"), plan,
         [g.reshape(sizes + block) for g in grads] + small + list(done),
         [like(block, F32)] * n + [like(x.shape, x.dtype) for x in small] + wide, [VMEM] * (n + 6),
-        order=(0, 1, 2) * 3 + bulk + (0, 1, 2) + rest * 2 + bulk * 2, through=through,
+        order=(0, 1, 2) * 2 + bulk + (0, 1, 2) * 2 + rest * 2 + bulk * 2, through=through,
     )
     return got[:n], [x.reshape(-1)[: y.size].reshape(y.shape).astype(F32) for x, y in zip(got[n : n + 3], sums)], got[n + 3 : -1], got[-1]
 
@@ -1276,8 +1306,8 @@
     down_bias,
     cotangent,
 ):
-    mixer_t, branch_t, output_t, stream_all, scale_all, down_pieces = fetch_first(
-        mixer_weight.T, branch_weight.T, output_weight.T, stream, scale_first, down_weight.T
+    mixer_t, branch_t, output_t, stream_all, scale_all, cot_all = fetch_first(
+        mixer_weight.T, branch_weight.T, output_weight.T, stream, scale_first, cotangent
     )
     inner = mixer_t.shape[0]
     stream_wide = stream.astype(F32)
@@ -1324,19 +1354,15 @@
     normed_second = first_out * inverse_second * (1.0 + scale_second)
 
     share = down_weight.shape[0] // (2 * TEAM)
-    second_all, cot_all, gate_t, up_t, down_t, gate_pre, up_pre = fetch_second(
-        normed_second.astype(BF16), cotangent, gate_weight.T, up_weight.T, down_pieces
-    )
     mine = (lax.axis_index("t") * 2 + lax.axis_index("col")) * share
     gate_b = lax.dynamic_slice(gate_bias, (mine,), (share,))
     up_b = lax.dynamic_slice(up_bias, (mine,), (share,))
 
-    gate_pre = gate_pre + gate_b
-    up_pre = up_pre + up_b
-    hidden, hidden_back = jax.vjp(lambda g, u: gelu_tanh(g) * u, gate_pre, up_pre)
-    hidden_low = hidden.astype(BF16)
+    second_all, gate_t, up_t, down_t, gate_slope, up_slope, hidden_low = fetch_second(
+        normed_second.astype(BF16), gate_weight.T, up_weight.T, down_weight.T, gate_b, up_b
+    )
     delta_hidden = dot_nn(cot_all, down_t)
-    delta_gate, delta_up = hidden_back(delta_hidden)
+    delta_gate, delta_up = delta_hidden * gate_slope, delta_hidden * up_slope
     gate_low, up_low = delta_gate.astype(BF16), delta_up.astype(BF16)
     down_part = dot_nt(hidden_low, down_t).astype(BF16)
     down_rows = lax.psum_scatter(down_part, "col", scatter_dimension=1, tiled=True)

time: 857 us -> 852 us (level)
    pallas_call x1, Pallas kernels: 129 us -> 108 us  [fetch_second(): pl.pallas_call(kernel, out_shape=(every, weight, weight, like((2, t, flee...]
    pallas_call x7, Pallas kernels: 299 us -> 314 us  [exchange(): pl.pallas_call(kernel, out_shape=tuple(out_shapes), in_specs=in_specs, ou...]
    unnamed x195 -> x193, local copies, waits for them, and re-layouts: 19.8 us -> 20.6 us
  transfers between devices with their start and end apart: 5 -> 5, of which waited for: 1 -> 1; matrix products, arithmetic and copies ran while one was open for 8% -> 10% of each run, Pallas kernels for 19% -> 19%
where the time goes in v2:
time: 852 us; the launch traced here: 840 us
  Pallas kernels  591 us (69%)
  matrix products  75.3 us (9%)
  waiting for transfers between devices  68.2 us (8%)
  other arithmetic  47.2 us (6%)
  local copies, waits for them, and re-layouts  39 us (5%)
  between operations  15.7 us (2%)
    pallas_call x7, Pallas kernels, exchange(): pl.pallas_call(kernel, out_shape=tuple(out_shapes), in_specs=in_specs, ou...  314 us
    pallas_call x1, Pallas kernels, send_second(): pl.pallas_call(kernel, out_shape=(like(block, F32), like(weight, BF16), l...  110 us
    pallas_call x1, Pallas kernels, fetch_second(): pl.pallas_call(kernel, out_shape=(every, weight, weight, like((2, t, flee...  108 us
    reduce_scatter x1, waiting for transfers between devices, on_device(): lax.psum_scatter(down_rows, ('t', 'row'), scatter_dimension=0, tiled=True)  68.2 us
    pallas_call x2, Pallas kernels, recurrence(): pl.pallas_call(kernel, out_shape=(like((rows, width), F32), like((8, widt...  36.9 us
    dot_general x14, matrix products, dot_nn(): return jnp.dot(a, b, preferred_element_type=F32)  33.6 us
    dot_general x14, matrix products, dot_nt(): return lax.dot_general(a, b, NT, preferred_element_type=F32)  28.6 us
    pallas_call x1, Pallas kernels, to_tokens(): pl.pallas_call(kernel, out_shape=(like((1, rows, 2 * width), BF16), like(...  21.6 us
  transfers between devices with their start and end apart: 5, of which 1 were waited for; matrix products, arithmetic and copies ran while one was open for 10% of the time, Pallas kernels for 19%

profile of v2, /device:TPU:0, one launch (start us, length us, event | category | flops | bytes accessed | tf_op | source)
XLA Modules:
  0.0 840.4 jit_solution(18254029956381031435)
XLA Ops:
  7.2 1.3 broadcast_in_dim.130.refs_4_
  8.5 149.6 %shard_map.398 = (bf16[4,2,160,2560]{3,2,1,0:T(8,128)(2,1)}, bf16[4,2,160,2560]{3,2,1,0:T(8,128)(2,1)}, bf16[2,4,2,160,1280]{4,3,2,1,0:T(8,128)(2,1)}, bf16[1,25...) custom-call(bf16[160,1280]{1,0:T(8,128)(2,1)} %bitcast.214, ...), custom_call_target="tpu_custom_call" | custom-call | tf_op jit(solution)/shard_map/pallas_call | solution.py:664
  159.0 1.7 fusion.3
  160.8 4.8 convolution_add_fusion.2
  165.6 2.5 collective-permute-start
  168.4 1.4 dynamic_slice.6
  169.8 1.3 dynamic_slice.7
  171.2 1.3 add_convert_fusion.1
  174.8 3.1 convert_multiply_fusion.6
  178.5 13.5 %states.1 = (f32[256,1280]{1,0:T(8,128)}, f32[8,1280]{1,0:T(8,128)}) custom-call(f32[256,1280]{1,0:T(8,128)} %get-tuple-element.142.r_ref, f32[256,1280]{1,0:T(8,128)} %get-tuple-element.141.s_ref, f32[8,1280]{1,0:T(8,128)} %broadcast_in_dim_broadcast_in_dim.3.lead_ref), custom_call_target="tpu_custom_call" | custom-call | tf_op jit(solution)/shard_map/states/pallas_call | solution.py:825
  192.0 6.4 multiply_convert_fusion.3
  198.4 5.0 convolution_convert_fusion.4
  203.5 1.2 maximum_bitcast_fusion.refs_0_
  204.7 13.3 %shard_map.399 = f32[256,1280]{1,0:T(8,128)} custom-call(bf16[2,1,256,1280]{3,2,1,0:T(8,128)(2,1)} %maximum_bitcast_fusion.refs_0_), custom_call_target="tpu_custom_call" | custom-call | tf_op jit(solution)/shard_map/pallas_call | solution.py:664
  218.0 1.7 multiply_reduce_fusion.9
  220.8 9.5 %shard_map.400 = f32[2,256,128]{2,1,0:T(8,128)} custom-call(f32[256,128]{1,0:T(8,128)} %pad_maximum_fusion.6.refs_0_), custom_call_target="tpu_custom_call" | custom-call | tf_op jit(solution)/shard_map/pallas_call | solution.py:664
  230.3 1.0 add_bitcast_fusion.2
  232.1 1.0 multiply_convert_fusion.2.n_ref
  233.1 108.3 %fetch_second.1 = (bf16[4,2,256,2560]{3,2,1,0:T(8,128)(2,1)}, bf16[1,480,2560]{2,1,0:T(8,128)(2,1)}, bf16[1,480,2560]{2,1,0:T(8,128)(2,1)}, bf16[2,4,2,160,480]{...) custom-call(bf16[256,1280]{1,0:T(8,128)(2,1)} %multiply_convert_fusion.2.n_ref, ...), custom_call_target="tpu_custom_call" | custom-call | tf_op jit(solution)/shard_map/fetch_second/pallas_call | solution.py:984
  341.4 10.3 %convolution_convert_fusion.refs_7_ = bf16[2048,2560]{1,0:T(8,128)(2,1)} fusion(bf16[2048,480]{1,0:T(8,128)(2,1)} %get-tuple-element.71.refs_2_, bf16[2560,480]{1,0:T(8,128)(2,1)} %bitcast.230), kind=kOutput, calls=%fused_computation | convolution fusion | flops 5038407680 | bytes 14909440 | tf_op jit(solution)/shard_map/dot_general | solution.py:31
  351.8 1.7 copy-done.82
  353.4 14.5 %multiply_reduce_fusion = (f32[480]{0:T(512)}, f32[480]{0:T(512)}, bf16[2048,480]{1,0:T(8,128)(2,1)}, bf16[2048,480]{1,0:T(8,128)(2,1)}) fusion(f32[2048,480]{1,0:T(8,128)} %get-tuple-element.70, f32[2048,480]{1,0:T(8,128)} %get-tuple-element.69, bf16[2048,2560]{1,0:T(8,128)(2,1)} %bitcast.189, bf16[2560,480]{1,0:T(8,128)(2,1)S(1)} %bitcast.231), kind=kOutput, calls=%fused_computation.29 | convolution fusion | flops 5039062016 | bytes 24743680 | tf_op jit(solution)/shard_map/dot_general | solution.py:27
  367.9 109.7 %send_second.1 = (f32[256,1280]{1,0:T(8,128)}, bf16[480,1280]{1,0:T(8,128)(2,1)}, bf16[480,1280]{1,0:T(8,128)(2,1)}, bf16[4,2,160,480]{3,2,1,0:T(8,128)(2,1)}) custom-call(bf16[2048,480]{1,0:T(8,128)(2,1)} %get-tuple-element.130.refs_0_, bf16[2048,480]{1,0:T(8,128)(2,1)} %get-tuple-element.131.refs_1_, bf16[2048,480]{1,0:T(8,128)(2,1)} %get-tuple-element.71.refs_2_, ...), custom_call_target="tpu_custom_call" | custom-call | tf_op jit(solution)/shard_map/send_second/pallas_call | solution.py:1142
  477.6 2.1 multiply_reduce_fusion.2
  480.5 3.2 shard_map.401
  483.6 1.0 add_bitcast_fusion.1
  485.4 1.1 copy-done.8
  487.4 21.6 %to_tokens.1 = (bf16[1,256,2560]{2,1,0:T(8,128)(2,1)}, bf16[256,1280]{1,0:T(8,128)(2,1)}, bf16[2,256,1280]{2,1,0:T(8,128)(2,1)}) custom-call(bf16[256,1280]{1,0:T(8,128)(2,1)} %convert_element_type.124.block_ref, bf16[256,1280]{1,0:T(8,128)(2,1)} %copy-done.38), custom_call_target="tpu_custom_call" | custom-call | tf_op jit(solution)/shard_map/to_tokens/pallas_call | solution.py:1214
  508.9 1.7 broadcast_select_fusion.1
  510.8 3.6 convolution_convert_fusion.1
  517.2 1.2 pad_maximum_fusion.1.refs_1_
  519.1 1.1 concatenate.37.r_ref
  522.1 8.4 %fusion.166 = (f32[1280]{0:T(1024)}, bf16[256,1280]{1,0:T(8,128)(2,1)}, f32[256,1280]{1,0:T(8,128)}) fusion(f32[256,1280]{1,0:T(8,128)} %get-tuple-element.170, f32[256,1280]{1,0:T(8,128)} %get-tuple-element.64, bf16[2560,1280]{1,0:T(8,128)(2,1)} %bitcast.229, bf16[1,256,2560]{2,1,0:T(8,128)(2,1)} %get-tuple-element.77), kind=kOutput, calls=%fused_computation.307 | convolution fusion | flops 1685584640 | bytes 12456960 | tf_op jit(solution)/shard_map/dot_general | solution.py:27
  531.2 23.5 %back_states.1 = (f32[256,1280]{1,0:T(8,128)}, f32[8,1280]{1,0:T(8,128)}) custom-call(f32[256,1280]{1,0:T(8,128)} %concatenate.37.r_ref, f32[256,1280]{1,0:T(8,128)} %get-tuple-element.134.s_ref, f32[8,1280]{1,0:T(8,128)} %broadcast_in_dim.140.lead_ref), custom_call_target="tpu_custom_call" | custom-call | tf_op jit(solution)/shard_map/back_states/pallas_call | solution.py:825
  554.7 5.4 multiply_reduce_fusion.7
  561.2 1.0 copy-done.34
  564.5 1.0 copy-done.35
  566.3 6.8 multiply_reduce_fusion.5
  573.6 1.6 collective-permute-start.1
  577.7 1.2 pad_maximum_fusion.3
  578.9 1.5 pad_add_fusion
  580.4 3.3 fusion.173
  585.3 5.5 fusion
  590.9 1.2 maximum_bitcast_fusion.1.refs_0_
  592.1 16.1 %shard_map.402 = (f32[256,1280]{1,0:T(8,128)}, bf16[256,1280]{1,0:T(8,128)(2,1)}, bf16[2,256,1280]{2,1,0:T(8,128)(2,1)}, bf16[2,256,1280]{2,1,0:T(8,128)(2,1)}) custom-call(bf16[2,1,256,1280]{3,2,1,0:T(8,128)(2,1)} %maximum_bitcast_fusion.1.refs_0_, bf16[2,256,1280]{2,1,0:T(8,128)(2,1)} %pad_maximum_fusion.1.refs_1_, ...), custom_call_target="tpu_custom_call" | custom-call | tf_op jit(solution)/shard_map/pallas_call | solution.py:664
  608.2 2.0 fusion.26
  611.0 12.1 %shard_map.404 = f32[2,256,128]{2,1,0:T(8,128)} custom-call(f32[256,128]{1,0:T(8,128)} %broadcast_in_dim.141.refs_0_), custom_call_target="tpu_custom_call" | custom-call | tf_op jit(solution)/shard_map/pallas_call | solution.py:664
  623.7 1.0 add_bitcast_fusion
  624.8 1.3 broadcast_select_fusion.3
  626.3 3.6 convolution_convert_fusion.3
  630.0 3.7 convolution_convert_fusion.2
  633.7 1.5 fusion.25
  635.2 1.9 convert_bitcast_fusion.1
  637.1 68.2 %reduce-scatter.6.cloned.1.call-done.refs_8_ = bf16[256,1280]{1,0:T(8,128)(2,1)} async-done(((bf16[2048,1280]{1,0:T(8,128)(2,1)}), bf16[256,1280]{1,0:T(8,128)(2,1)}) %reduce-scatter.6.cloned.1.call-update) | async-done | bytes 655376 | tf_op jit(solution)/shard_map/reduce_scatter | solution.py:1377
  705.3 110.6 %shard_map.403 = (f32[160,1280]{1,0:T(8,128)}, f32[160,1280]{1,0:T(8,128)}, f32[4,2,2,8,256]{4,3,2,1,0:T(8,128)}, f32[4,2,2,8,128]{4,3,2,1,0:T(8,128)}, bf16[4,2...) custom-call(bf16[4,2,160,1280]{3,2,1,0:T(8,128)(2,1)} %bitcast.193, ...), custom_call_target="tpu_custom_call", output_to_operand_aliasing={{8}: (8, {})} | custom-call | tf_op jit(solution)/shard_map/pallas_call | solution.py:664
  815.9 1.0 copy.113
  818.1 1.4 fusion.172
  820.2 3.1 fusion.169
  823.3 1.0 add_convert_fusion
  826.9 1.4 copy.160
  828.3 1.1 copy-done.32
  829.5 1.4 copy.161
  830.9 1.1 copy-done.31
  832.0 1.4 copy.162
  (284 shorter events, 29.0 us)
Async XLA Ops:
  7.2 472.5 %reduce-scatter.4.cloned.1.call-start = ((), (), s32[]{:S(2)}) async-start(), calls=%async_computation.3 | async-start | bytes 15728640 | tf_op jit(solution)/shard_map/reduce_scatter | solution.py:1368
  158.1 2.6 copy-start.18
  158.1 2.6 copy-start.86
  159.0 33.0 %copy-start.49 = (f32[2560]{0:T(1024)}, f32[2560]{0:T(1024)S(1)}, u32[]{:S(2)}) copy-start(f32[2560]{0:T(1024)S(1)} %add.258) | copy-start | bytes 30724
  160.7 31.3 %copy-start.78 = (f32[256]{0:T(256)}, f32[256]{0:T(256)S(1)}, u32[]{:S(2)}) copy-start(f32[256]{0:T(256)S(1)} %add_rsqrt_fusion) | copy-start | bytes 3076
  160.7 7.5 copy-start.57
  160.7 7.6 copy-start.51
  160.8 7.6 copy-start.64
  160.8 10.4 %copy-start.61 = (f32[1280]{0:T(1024)S(1)}, f32[1280]{0:T(1024)}, u32[]{:S(2)}) copy-start(f32[1280]{0:T(1024)} %param.30) | copy-start | bytes 15364
  165.6 12.3 %copy-start.14 = (f32[256,1280]{1,0:T(8,128)}, f32[256,1280]{1,0:T(8,128)S(1)}, u32[]{:S(2)}) copy-start(f32[256,1280]{1,0:T(8,128)S(1)} %convolution_add_fusion.2) | copy-start | bytes 3932164
  165.6 6.8 copy-start.24
  165.6 5.5 collective-permute-start
  168.2 4.5 copy-start.66
  168.2 4.5 copy-start.68
  168.2 4.4 copy-start.70
  168.3 6.5 copy-start.74
  168.3 4.3 copy-start.43
  168.3 4.3 copy-start.45
  168.4 4.5 copy-start.72
  172.4 2.3 copy-start.4
  173.8 4.1 copy-start.6
  174.7 3.2 copy-start.2
  178.5 13.5 %copy-start.87 = (f32[1280]{0:T(1024)S(1)}, f32[1280]{0:T(1024)}, u32[]{:S(2)}) copy-start(f32[1280]{0:T(1024)} %param.26) | copy-start | bytes 15364
  198.4 5.0 copy-start.38
  204.7 13.3 %copy-start.12 = (bf16[256,1280]{1,0:T(8,128)(2,1)S(1)}, bf16[256,1280]{1,0:T(8,128)(2,1)}, u32[]{:S(2)}) copy-start(bf16[256,1280]{1,0:T(8,128)(2,1)} %refs_3_.1) | copy-start | bytes 1966084
  204.7 13.3 %copy-start.62 = (f32[1280]{0:T(1024)S(1)}, f32[1280]{0:T(1024)}, u32[]{:S(2)}) copy-start(f32[1280]{0:T(1024)} %param.37) | copy-start | bytes 15364
  219.7 13.4 %copy-start = (f32[256,1280]{1,0:T(8,128)}, f32[256,1280]{1,0:T(8,128)S(1)}, u32[]{:S(2)}) copy-start(f32[256,1280]{1,0:T(8,128)S(1)} %get-tuple-element.129) | copy-start | bytes 3932164
  232.1 109.3 %copy-start.58 = (f32[256]{0:T(256)}, f32[256]{0:T(256)S(1)}, u32[]{:S(2)}) copy-start(f32[256]{0:T(256)S(1)} %get-tuple-element.115) | copy-start | bytes 3076
  351.7 283.4 %reduce-scatter.8.cloned.1.call-start = ((), (), s32[]{:S(2)}) async-start(), calls=%async_computation.5 | async-start | bytes 3686400 | tf_op jit(solution)/shard_map/reduce_scatter | solution.py:1381
  480.4 4.3 copy-start.1
  480.4 4.3 copy-start.17
  480.4 4.3 copy-start.21
  480.4 4.3 copy-start.59
  480.4 4.3 copy-start.77
  514.5 190.8 %reduce-scatter.6.cloned.1.call-start = ((), (), s32[]{:S(2)}) async-start(), calls=%async_computation.4 | async-start | bytes 5898240 | tf_op jit(solution)/shard_map/reduce_scatter | solution.py:1377
  519.1 2.6 copy-start.81
  519.1 2.7 copy-start.80
  531.2 23.5 %copy-start.3 = (f32[256,1280]{1,0:T(8,128)S(1)}, f32[256,1280]{1,0:T(8,128)}, u32[]{:S(2)}) copy-start(f32[256,1280]{1,0:T(8,128)} %copy-done.2) | copy-start | bytes 3932164
  531.2 23.5 %copy-start.5 = (bf16[256,1280]{1,0:T(8,128)(2,1)S(1)}, bf16[256,1280]{1,0:T(8,128)(2,1)}, u32[]{:S(2)}) copy-start(bf16[256,1280]{1,0:T(8,128)(2,1)} %copy-done.4) | copy-start | bytes 1966084
  531.2 23.5 %copy-start.48 = (f32[1280]{0:T(1024)S(1)}, f32[1280]{0:T(1024)}, u32[]{:S(2)}) copy-start(f32[1280]{0:T(1024)} %param.34) | copy-start | bytes 15364
  531.2 23.5 %copy-start.75 = (pred[256]{0:T(512)(128)(4,1)S(1)}, pred[256]{0:T(512)(128)(4,1)}, u32[]{:S(2)}) copy-start(pred[256]{0:T(512)(128)(4,1)} %copy-done.74) | copy-start | bytes 772
  554.7 5.4 copy-start.25
  566.3 6.8 copy-start.44
  566.3 6.8 copy-start.46
  566.3 6.8 copy-start.73
  573.6 10.2 %collective-permute-start.1 = (f32[3,1280]{1,0:T(4,128)S(1)}, f32[3,1280]{1,0:T(4,128)S(1)}, u32[]{:S(2)}, u32[]{:S(2)}) collective-permute-start(f32[3,1280]{1,0:T(4,128)S(1)} %pad_add_fusion.1), channel_id=1, source_target_pairs={{1,0},{4,1},{5,4},{8,5},{9,8},{12,9},{13,12},{16,13},{17,16},{20,1... | collective-permute-start | bytes 46088 | tf_op jit(solution)/shard_map/ppermute | solution.py:847
  575.6 4.8 slice-start
  577.7 2.7 slice-start.1
  580.4 3.4 copy-start.65
  580.4 3.4 copy-start.15
  584.1 6.8 copy-start.28
  592.1 16.1 %copy-start.13 = (bf16[256,1280]{1,0:T(8,128)(2,1)S(1)}, bf16[256,1280]{1,0:T(8,128)(2,1)}, u32[]{:S(2)}) copy-start(bf16[256,1280]{1,0:T(8,128)(2,1)} %refs_3_.1) | copy-start | bytes 1966084
  592.1 16.1 %copy-start.60 = (f32[256]{0:T(256)S(1)}, f32[256]{0:T(256)}, u32[]{:S(2)}) copy-start(f32[256]{0:T(256)} %get-tuple-element.114) | copy-start | bytes 3076
  608.2 2.0 copy-start.56
  608.2 16.6 %copy-start.11 = (bf16[256,2560]{1,0:T(8,128)(2,1)S(1)}, bf16[256,2560]{1,0:T(8,128)(2,1)}, u32[]{:S(2)}) copy-start(bf16[256,2560]{1,0:T(8,128)(2,1)} %copy-done.10) | copy-start | bytes 3932164
  626.3 3.6 copy-start.83
  630.0 3.7 copy-start.9
  630.0 3.7 copy-start.16
  630.0 3.7 copy-start.76
  820.2 3.1 copy-start.20
  820.2 3.1 copy-start.63
  824.6 2.3 copy-start.33
  826.9 2.6 copy-start.32
  829.5 2.6 copy-start.31
  (31 other events, 37.1 us)
Sparse Core Ops, SparseCore 0:
  351.8 16.6 reduce-scatter.3
  514.6 85.1 reduce-scatter.7
  603.3 101.8 reduce-scatter.5

commit v3 on v2

--- a/solution.py
+++ b/solution.py
@@ -592,14 +592,15 @@
             first, first, second, second, pltpu.SemaphoreType.DMA,
         ]
 
-    def begin(self):
+    def begin(self, core=None):
         for tag in grid_of(("t", "col"), True):
             to = peer_of("t", tag[0]), peer_of("col", tag[1])
+            condition = None if core is None else to[1] == core
             for k in offsets("f"):
                 at = (k - 1,) + tag
                 self.push(
                     self.src.at[(peer_of("f", k),) + to], self.come.at[(k - 1,) + to],
-                    self.send.at[at], self.recv.at[at], {"f": peer_of("f", k)},
+                    self.send.at[at], self.recv.at[at], {"f": peer_of("f", k)}, condition,
                 )
 
     def stage(self, wave):
@@ -1104,11 +1105,13 @@
         team = sums.order(1)
         fetch(cot_ref, 0).start()
         greet(team_peers())
+        turn(h_ref, ht_ref)
+        lax.fori_loop(0, wide // tile // 2, down_gradients, 0)
+        d_job.begin(0)
         block_of(away[0])
-        turn(h_ref, ht_ref)
+        lax.fori_loop(wide // tile // 2, wide // tile, down_gradients, 0)
+        d_job.begin(1)
         sums.step(2, away[0])
-        lax.fori_loop(0, wide // tile, down_gradients, 0)
-        d_job.begin()
         block_of(away[1])
         block_of(home[0])
         sums.step(2, away[1])

time: 852 us -> 858 us (level)
  transfers between devices with their start and end apart: 5 -> 5, of which waited for: 1 -> 1; matrix products, arithmetic and copies ran while one was open for 10% -> 10% of each run, Pallas kernels for 19% -> 20%
where the time goes in v3:
time: 858 us; the launch traced here: 846 us
  Pallas kernels  597 us (70%)
  matrix products  75.3 us (9%)
  waiting for transfers between devices  68.3 us (8%)
  other arithmetic  47.1 us (5%)
  local copies, waits for them, and re-layouts  39 us (5%)
  between operations  15.7 us (2%)
    pallas_call x7, Pallas kernels, exchange(): pl.pallas_call(kernel, out_shape=tuple(out_shapes), in_specs=in_specs, ou...  314 us
    pallas_call x1, Pallas kernels, send_second(): pl.pallas_call(kernel, out_shape=(like(block, F32), like(weight, BF16), l...  116 us
    pallas_call x1, Pallas kernels, fetch_second(): pl.pallas_call(kernel, out_shape=(every, weight, weight, like((2, t, flee...  108 us
    reduce_scatter x1, waiting for transfers between devices, on_device(): lax.psum_scatter(down_rows, ('t', 'row'), scatter_dimension=0, tiled=True)  68.2 us
    pallas_call x2, Pallas kernels, recurrence(): pl.pallas_call(kernel, out_shape=(like((rows, width), F32), like((8, widt...  37 us
    dot_general x14, matrix products, dot_nn(): return jnp.dot(a, b, preferred_element_type=F32)  33.5 us
    dot_general x14, matrix products, dot_nt(): return lax.dot_general(a, b, NT, preferred_element_type=F32)  28.6 us
    pallas_call x1, Pallas kernels, to_tokens(): pl.pallas_call(kernel, out_shape=(like((1, rows, 2 * width), BF16), like(...  21.6 us
  transfers between devices with their start and end apart: 5, of which 1 were waited for; matrix products, arithmetic and copies ran while one was open for 10% of the time, Pallas kernels for 20%

profile of v3, /device:TPU:0, one launch (start us, length us, event | category | flops | bytes accessed | tf_op | source)
XLA Modules:
  0.0 846.4 jit_solution(4306630125198968298)
XLA Ops:
  7.2 1.3 broadcast_in_dim.130.refs_4_
  8.5 149.6 %shard_map.398 = (bf16[4,2,160,2560]{3,2,1,0:T(8,128)(2,1)}, bf16[4,2,160,2560]{3,2,1,0:T(8,128)(2,1)}, bf16[2,4,2,160,1280]{4,3,2,1,0:T(8,128)(2,1)}, bf16[1,25...) custom-call(bf16[160,1280]{1,0:T(8,128)(2,1)} %bitcast.214, ...), custom_call_target="tpu_custom_call" | custom-call | tf_op jit(solution)/shard_map/pallas_call | solution.py:665
  159.0 1.7 fusion.3
  160.8 4.8 convolution_add_fusion.2
  165.6 2.5 collective-permute-start
  168.4 1.4 dynamic_slice.6
  169.8 1.3 dynamic_slice.7
  171.2 1.3 add_convert_fusion.1
  174.8 3.1 convert_multiply_fusion.6
  178.5 13.5 %states.1 = (f32[256,1280]{1,0:T(8,128)}, f32[8,1280]{1,0:T(8,128)}) custom-call(f32[256,1280]{1,0:T(8,128)} %get-tuple-element.142.r_ref, f32[256,1280]{1,0:T(8,128)} %get-tuple-element.141.s_ref, f32[8,1280]{1,0:T(8,128)} %broadcast_in_dim_broadcast_in_dim.3.lead_ref), custom_call_target="tpu_custom_call" | custom-call | tf_op jit(solution)/shard_map/states/pallas_call | solution.py:826
  192.0 6.4 multiply_convert_fusion.3
  198.4 5.0 convolution_convert_fusion.4
  203.5 1.2 maximum_bitcast_fusion.refs_0_
  204.7 13.3 %shard_map.399 = f32[256,1280]{1,0:T(8,128)} custom-call(bf16[2,1,256,1280]{3,2,1,0:T(8,128)(2,1)} %maximum_bitcast_fusion.refs_0_), custom_call_target="tpu_custom_call" | custom-call | tf_op jit(solution)/shard_map/pallas_call | solution.py:665
  218.0 1.7 multiply_reduce_fusion.9
  220.8 9.5 %shard_map.400 = f32[2,256,128]{2,1,0:T(8,128)} custom-call(f32[256,128]{1,0:T(8,128)} %pad_maximum_fusion.6.refs_0_), custom_call_target="tpu_custom_call" | custom-call | tf_op jit(solution)/shard_map/pallas_call | solution.py:665
  230.3 1.0 add_bitcast_fusion.2
  232.1 1.0 multiply_convert_fusion.2.n_ref
  233.1 108.3 %fetch_second.1 = (bf16[4,2,256,2560]{3,2,1,0:T(8,128)(2,1)}, bf16[1,480,2560]{2,1,0:T(8,128)(2,1)}, bf16[1,480,2560]{2,1,0:T(8,128)(2,1)}, bf16[2,4,2,160,480]{...) custom-call(bf16[256,1280]{1,0:T(8,128)(2,1)} %multiply_convert_fusion.2.n_ref, ...), custom_call_target="tpu_custom_call" | custom-call | tf_op jit(solution)/shard_map/fetch_second/pallas_call | solution.py:985
  341.4 10.3 %convolution_convert_fusion.refs_7_ = bf16[2048,2560]{1,0:T(8,128)(2,1)} fusion(bf16[2048,480]{1,0:T(8,128)(2,1)} %get-tuple-element.71.refs_2_, bf16[2560,480]{1,0:T(8,128)(2,1)} %bitcast.230), kind=kOutput, calls=%fused_computation | convolution fusion | flops 5038407680 | bytes 14909440 | tf_op jit(solution)/shard_map/dot_general | solution.py:31
  351.8 1.7 copy-done.82
  353.4 14.5 %multiply_reduce_fusion = (f32[480]{0:T(512)}, f32[480]{0:T(512)}, bf16[2048,480]{1,0:T(8,128)(2,1)}, bf16[2048,480]{1,0:T(8,128)(2,1)}) fusion(f32[2048,480]{1,0:T(8,128)} %get-tuple-element.70, f32[2048,480]{1,0:T(8,128)} %get-tuple-element.69, bf16[2048,2560]{1,0:T(8,128)(2,1)} %bitcast.189, bf16[2560,480]{1,0:T(8,128)(2,1)S(1)} %bitcast.231), kind=kOutput, calls=%fused_computation.29 | convolution fusion | flops 5039062016 | bytes 24743680 | tf_op jit(solution)/shard_map/dot_general | solution.py:27
  367.9 115.6 %send_second.1 = (f32[256,1280]{1,0:T(8,128)}, bf16[480,1280]{1,0:T(8,128)(2,1)}, bf16[480,1280]{1,0:T(8,128)(2,1)}, bf16[4,2,160,480]{3,2,1,0:T(8,128)(2,1)}) custom-call(bf16[2048,480]{1,0:T(8,128)(2,1)} %get-tuple-element.130.refs_0_, bf16[2048,480]{1,0:T(8,128)(2,1)} %get-tuple-element.131.refs_1_, bf16[2048,480]{1,0:T(8,128)(2,1)} %get-tuple-element.71.refs_2_, ...), custom_call_target="tpu_custom_call" | custom-call | tf_op jit(solution)/shard_map/send_second/pallas_call | solution.py:1145
  483.6 2.1 multiply_reduce_fusion.2
  486.4 3.2 shard_map.401
  489.6 1.0 add_bitcast_fusion.1
  491.3 1.1 copy-done.8
  493.3 21.6 %to_tokens.1 = (bf16[1,256,2560]{2,1,0:T(8,128)(2,1)}, bf16[256,1280]{1,0:T(8,128)(2,1)}, bf16[2,256,1280]{2,1,0:T(8,128)(2,1)}) custom-call(bf16[256,1280]{1,0:T(8,128)(2,1)} %convert_element_type.124.block_ref, bf16[256,1280]{1,0:T(8,128)(2,1)} %copy-done.38), custom_call_target="tpu_custom_call" | custom-call | tf_op jit(solution)/shard_map/to_tokens/pallas_call | solution.py:1217
  514.9 1.7 broadcast_select_fusion.1
  516.8 3.6 convolution_convert_fusion.1
  523.2 1.2 pad_maximum_fusion.1.refs_1_
  525.1 1.1 concatenate.37.r_ref
  528.1 8.4 fusion.166
  537.1 23.6 %back_states.1 = (f32[256,1280]{1,0:T(8,128)}, f32[8,1280]{1,0:T(8,128)}) custom-call(f32[256,1280]{1,0:T(8,128)} %concatenate.37.r_ref, f32[256,1280]{1,0:T(8,128)} %get-tuple-element.134.s_ref, f32[8,1280]{1,0:T(8,128)} %broadcast_in_dim.140.lead_ref), custom_call_target="tpu_custom_call" | custom-call | tf_op jit(solution)/shard_map/back_states/pallas_call | solution.py:826
  560.7 5.4 multiply_reduce_fusion.7
  567.3 1.0 copy-done.34
  570.5 1.0 copy-done.35
  572.3 6.8 multiply_reduce_fusion.5
  579.7 1.6 collective-permute-start.1
  583.8 1.2 pad_maximum_fusion.3
  585.0 1.5 pad_add_fusion
  586.5 3.3 fusion.173
  591.3 5.5 fusion
  597.0 1.2 maximum_bitcast_fusion.1.refs_0_
  598.1 16.1 %shard_map.402 = (f32[256,1280]{1,0:T(8,128)}, bf16[256,1280]{1,0:T(8,128)(2,1)}, bf16[2,256,1280]{2,1,0:T(8,128)(2,1)}, bf16[2,256,1280]{2,1,0:T(8,128)(2,1)}) custom-call(bf16[2,1,256,1280]{3,2,1,0:T(8,128)(2,1)} %maximum_bitcast_fusion.1.refs_0_, bf16[2,256,1280]{2,1,0:T(8,128)(2,1)} %pad_maximum_fusion.1.refs_1_, ...), custom_call_target="tpu_custom_call" | custom-call | tf_op jit(solution)/shard_map/pallas_call | solution.py:665
  614.3 1.9 fusion.26
  617.0 12.0 %shard_map.404 = f32[2,256,128]{2,1,0:T(8,128)} custom-call(f32[256,128]{1,0:T(8,128)} %broadcast_in_dim.141.refs_0_), custom_call_target="tpu_custom_call" | custom-call | tf_op jit(solution)/shard_map/pallas_call | solution.py:665
  629.7 1.0 add_bitcast_fusion
  630.8 1.3 broadcast_select_fusion.3
  632.3 3.6 convolution_convert_fusion.3
  636.0 3.7 convolution_convert_fusion.2
  639.7 1.5 fusion.25
  641.2 1.9 convert_bitcast_fusion.1
  643.1 68.2 %reduce-scatter.6.cloned.1.call-done.refs_8_ = bf16[256,1280]{1,0:T(8,128)(2,1)} async-done(((bf16[2048,1280]{1,0:T(8,128)(2,1)}), bf16[256,1280]{1,0:T(8,128)(2,1)}) %reduce-scatter.6.cloned.1.call-update) | async-done | bytes 655376 | tf_op jit(solution)/shard_map/reduce_scatter | solution.py:1380
  711.3 110.6 %shard_map.403 = (f32[160,1280]{1,0:T(8,128)}, f32[160,1280]{1,0:T(8,128)}, f32[4,2,2,8,256]{4,3,2,1,0:T(8,128)}, f32[4,2,2,8,128]{4,3,2,1,0:T(8,128)}, bf16[4,2...) custom-call(bf16[4,2,160,1280]{3,2,1,0:T(8,128)(2,1)} %bitcast.193, ...), custom_call_target="tpu_custom_call", output_to_operand_aliasing={{8}: (8, {})} | custom-call | tf_op jit(solution)/shard_map/pallas_call | solution.py:665
  821.9 1.0 copy.113
  824.1 1.4 fusion.172
  826.2 3.1 fusion.169
  829.3 1.0 add_convert_fusion
  832.9 1.4 copy.160
  834.3 1.1 copy-done.32
  835.5 1.4 copy.161
  836.9 1.1 copy-done.31
  838.0 1.4 copy.162
  (284 shorter events, 29.0 us)
Async XLA Ops:
  7.2 478.4 %reduce-scatter.4.cloned.1.call-start = ((), (), s32[]{:S(2)}) async-start(), calls=%async_computation.3 | async-start | bytes 15728640 | tf_op jit(solution)/shard_map/reduce_scatter | solution.py:1371
  158.1 2.6 copy-start.18
  158.1 2.6 copy-start.86
  159.0 33.0 %copy-start.49 = (f32[2560]{0:T(1024)}, f32[2560]{0:T(1024)S(1)}, u32[]{:S(2)}) copy-start(f32[2560]{0:T(1024)S(1)} %add.258) | copy-start | bytes 30724
  160.7 31.3 %copy-start.78 = (f32[256]{0:T(256)}, f32[256]{0:T(256)S(1)}, u32[]{:S(2)}) copy-start(f32[256]{0:T(256)S(1)} %add_rsqrt_fusion) | copy-start | bytes 3076
  160.7 7.5 copy-start.57
  160.7 7.6 copy-start.51
  160.8 7.6 copy-start.64
  160.8 10.4 %copy-start.61 = (f32[1280]{0:T(1024)S(1)}, f32[1280]{0:T(1024)}, u32[]{:S(2)}) copy-start(f32[1280]{0:T(1024)} %param.30) | copy-start | bytes 15364
  165.6 12.3 %copy-start.14 = (f32[256,1280]{1,0:T(8,128)}, f32[256,1280]{1,0:T(8,128)S(1)}, u32[]{:S(2)}) copy-start(f32[256,1280]{1,0:T(8,128)S(1)} %convolution_add_fusion.2) | copy-start | bytes 3932164
  165.6 6.8 copy-start.24
  165.6 5.5 collective-permute-start
  168.2 4.5 copy-start.66
  168.2 4.5 copy-start.68
  168.2 4.4 copy-start.70
  168.3 6.5 copy-start.74
  168.3 4.3 copy-start.43
  168.3 4.3 copy-start.45
  168.4 4.5 copy-start.72
  172.4 2.3 copy-start.4
  173.8 4.1 copy-start.6
  174.7 3.2 copy-start.2
  178.5 13.5 %copy-start.87 = (f32[1280]{0:T(1024)S(1)}, f32[1280]{0:T(1024)}, u32[]{:S(2)}) copy-start(f32[1280]{0:T(1024)} %param.26) | copy-start | bytes 15364
  198.4 5.0 copy-start.38
  204.7 13.3 %copy-start.12 = (bf16[256,1280]{1,0:T(8,128)(2,1)S(1)}, bf16[256,1280]{1,0:T(8,128)(2,1)}, u32[]{:S(2)}) copy-start(bf16[256,1280]{1,0:T(8,128)(2,1)} %refs_3_.1) | copy-start | bytes 1966084
  204.7 13.3 %copy-start.62 = (f32[1280]{0:T(1024)S(1)}, f32[1280]{0:T(1024)}, u32[]{:S(2)}) copy-start(f32[1280]{0:T(1024)} %param.37) | copy-start | bytes 15364
  219.7 13.4 %copy-start = (f32[256,1280]{1,0:T(8,128)}, f32[256,1280]{1,0:T(8,128)S(1)}, u32[]{:S(2)}) copy-start(f32[256,1280]{1,0:T(8,128)S(1)} %get-tuple-element.129) | copy-start | bytes 3932164
  232.1 109.3 %copy-start.58 = (f32[256]{0:T(256)}, f32[256]{0:T(256)S(1)}, u32[]{:S(2)}) copy-start(f32[256]{0:T(256)S(1)} %get-tuple-element.115) | copy-start | bytes 3076
  351.7 289.4 %reduce-scatter.8.cloned.1.call-start = ((), (), s32[]{:S(2)}) async-start(), calls=%async_computation.5 | async-start | bytes 3686400 | tf_op jit(solution)/shard_map/reduce_scatter | solution.py:1384
  486.4 4.3 copy-start.1
  486.4 4.3 copy-start.17
  486.4 4.3 copy-start.21
  486.4 4.3 copy-start.59
  486.4 4.3 copy-start.77
  520.4 190.9 %reduce-scatter.6.cloned.1.call-start = ((), (), s32[]{:S(2)}) async-start(), calls=%async_computation.4 | async-start | bytes 5898240 | tf_op jit(solution)/shard_map/reduce_scatter | solution.py:1380
  525.0 2.6 copy-start.81
  525.0 2.7 copy-start.80
  537.1 23.6 %copy-start.3 = (f32[256,1280]{1,0:T(8,128)S(1)}, f32[256,1280]{1,0:T(8,128)}, u32[]{:S(2)}) copy-start(f32[256,1280]{1,0:T(8,128)} %copy-done.2) | copy-start | bytes 3932164
  537.1 23.6 %copy-start.5 = (bf16[256,1280]{1,0:T(8,128)(2,1)S(1)}, bf16[256,1280]{1,0:T(8,128)(2,1)}, u32[]{:S(2)}) copy-start(bf16[256,1280]{1,0:T(8,128)(2,1)} %copy-done.4) | copy-start | bytes 1966084
  537.1 23.6 %copy-start.48 = (f32[1280]{0:T(1024)S(1)}, f32[1280]{0:T(1024)}, u32[]{:S(2)}) copy-start(f32[1280]{0:T(1024)} %param.34) | copy-start | bytes 15364
  537.1 23.6 %copy-start.75 = (pred[256]{0:T(512)(128)(4,1)S(1)}, pred[256]{0:T(512)(128)(4,1)}, u32[]{:S(2)}) copy-start(pred[256]{0:T(512)(128)(4,1)} %copy-done.74) | copy-start | bytes 772
  560.7 5.4 copy-start.25
  572.3 6.8 copy-start.44
  572.3 6.8 copy-start.46
  572.3 6.8 copy-start.73
  579.7 10.2 %collective-permute-start.1 = (f32[3,1280]{1,0:T(4,128)S(1)}, f32[3,1280]{1,0:T(4,128)S(1)}, u32[]{:S(2)}, u32[]{:S(2)}) collective-permute-start(f32[3,1280]{1,0:T(4,128)S(1)} %pad_add_fusion.1), channel_id=1, source_target_pairs={{1,0},{4,1},{5,4},{8,5},{9,8},{12,9},{13,12},{16,13},{17,16},{20,1... | collective-permute-start | bytes 46088 | tf_op jit(solution)/shard_map/ppermute | solution.py:848
  581.6 4.8 slice-start
  583.8 2.7 slice-start.1
  586.5 3.4 copy-start.65
  586.5 3.4 copy-start.15
  590.1 6.8 copy-start.28
  598.1 16.1 %copy-start.13 = (bf16[256,1280]{1,0:T(8,128)(2,1)S(1)}, bf16[256,1280]{1,0:T(8,128)(2,1)}, u32[]{:S(2)}) copy-start(bf16[256,1280]{1,0:T(8,128)(2,1)} %refs_3_.1) | copy-start | bytes 1966084
  598.1 16.1 %copy-start.60 = (f32[256]{0:T(256)S(1)}, f32[256]{0:T(256)}, u32[]{:S(2)}) copy-start(f32[256]{0:T(256)} %get-tuple-element.114) | copy-start | bytes 3076
  614.2 2.0 copy-start.56
  614.2 16.6 %copy-start.11 = (bf16[256,2560]{1,0:T(8,128)(2,1)S(1)}, bf16[256,2560]{1,0:T(8,128)(2,1)}, u32[]{:S(2)}) copy-start(bf16[256,2560]{1,0:T(8,128)(2,1)} %copy-done.10) | copy-start | bytes 3932164
  632.3 3.6 copy-start.83
  636.0 3.7 copy-start.9
  636.0 3.7 copy-start.16
  636.0 3.7 copy-start.76
  826.2 3.1 copy-start.20
  826.2 3.1 copy-start.63
  830.6 2.3 copy-start.33
  832.9 2.6 copy-start.32
  835.5 2.6 copy-start.31
  (31 other events, 37.1 us)
Sparse Core Ops, SparseCore 0:
  351.8 16.6 reduce-scatter.3
  520.5 85.1 reduce-scatter.7
  609.3 101.9 reduce-scatter.5
